TPU v7x, 32 devices: a whole 2x2x4 slice. The times are simulated.
32 devices in a mesh: ma: 8 (over z, y), vert: 4 (over x, core).
Axes of the slice: x: 2, y: 2, z: 4, core: 2. Of those that a mesh axis runs over, the one named last changes fastest.
Arguments:
- trial_block: bfloat16 [128, 64, 4, 1024], P('vert', 'ma'), may hold values from -6 to 6
- legendre: bfloat16 [64, 2, 32, 1024], P('ma'), may hold values from -0.1875 to 0.1875
- order_slot: int32 [64], replicated, may hold values from 0 to 63, each once
- cycle_start: int32 [32], replicated, may hold values from 0 to 127
- cycle_count: int32 [32], replicated, may hold values from 0 to 128, as said below
- cycle_weight: float32 [32], replicated, may hold values from 4 to 32
Outputs:
- new_basis: bfloat16 [128, 64, 4, 1024], P('vert', 'ma')
- ritz_matrix: float32 [128, 128], replicated
Inputs may be any that keep to these rules, and one draw needn't show every extreme that they name: `cycle_count`: exactly 8 consecutive cycles have a nonzero count, and one of them has 128.
All inputs are finite; a program needn't handle non-finite values.
Results may differ from a plain program's by a relative error of at most 0.0073.
The roundings to bfloat16 on the way count: a program that leaves them out, or rounds other values in their place, can miss the bound.
Values may be sent and summed in bfloat16 or wider, within the bound.
A program may use at most 192 MiB of HBM per device.

v0:
```python
import math

import jax
import jax.numpy as jnp
from jax import lax
from jax.sharding import PartitionSpec as P


def combine_fields(products):
    first_kind = products[:, 0]
    second_kind = products[:, 1]
    return jnp.stack(
        [
            first_kind[..., 0] + second_kind[..., 3],
            first_kind[..., 1] - second_kind[..., 2],
            second_kind[..., 1] - first_kind[..., 2],
            -second_kind[..., 0] - first_kind[..., 3],
        ],
        axis=-1,
    )


def adjoint_terms(returned):
    gtc = returned[..., 0]
    gts = returned[..., 1]
    gpc = returned[..., 2]
    gps = returned[..., 3]
    first_kind = jnp.stack([gtc, gts, -gpc, -gps], axis=-1)
    second_kind = jnp.stack([-gps, gpc, -gts, gtc], axis=-1)
    return jnp.stack([first_kind, second_kind], axis=1)


def fourier_tables(order_slot, longitudes, orders_total):
    longitude = jnp.arange(longitudes, dtype=jnp.int32)
    phases = longitude[:, None] * order_slot[None, :] % longitudes
    angles = phases.astype(jnp.float32) * (2.0 * math.pi / longitudes)
    scale = 1.0 / math.sqrt(orders_total)
    return (
        (jnp.cos(angles) * scale).astype(jnp.bfloat16),
        (jnp.sin(angles) * scale).astype(jnp.bfloat16),
    )


def synthesize(trial_block, table_rows):
    orders_here = trial_block.shape[1]
    vectors = trial_block.shape[0]
    products = lax.dot_general(
        table_rows, trial_block, (((3,), (3,)), ((0,), (1,))), preferred_element_type=jnp.float32
    )
    fields = combine_fields(products).astype(jnp.bfloat16)
    return fields.reshape(orders_here, table_rows.shape[2], vectors * 4)


def cycle_transform(cycle_fields, cycle_first, order_slot, cycle_start, cycle_count, cycle_weight):
    orders_total, cycles_here, columns = cycle_fields.shape
    vectors = columns // 4
    longitudes = 2 * orders_total
    pieces = cycle_fields.reshape(orders_total, cycles_here, vectors, 4)
    cosine, sines = fourier_tables(order_slot, longitudes, orders_total)
    grid_values = jnp.einsum(
        "jo,orkc->rckj", cosine, pieces[..., 0::2], preferred_element_type=jnp.float32
    )
    grid_values = grid_values + jnp.einsum(
        "jo,orkc->rckj", sines, pieces[..., 1::2], preferred_element_type=jnp.float32
    )
    starts = lax.dynamic_slice_in_dim(cycle_start, cycle_first, cycles_here)
    counts = lax.dynamic_slice_in_dim(cycle_count, cycle_first, cycles_here)
    weights = lax.dynamic_slice_in_dim(cycle_weight, cycle_first, cycles_here)
    longitude = jnp.arange(longitudes, dtype=jnp.int32)
    inside = ((longitude[None, :] - starts[:, None]) % longitudes < counts[:, None]).astype(
        jnp.float32
    )
    factor = inside * weights[:, None]
    weighted = (grid_values * factor[:, None, None, :]).astype(jnp.bfloat16)
    back_cos = jnp.einsum("jo,rckj->orkc", cosine, weighted, preferred_element_type=jnp.float32)
    back_sin = jnp.einsum("jo,rckj->orkc", sines, weighted, preferred_element_type=jnp.float32)
    returned = jnp.stack(
        [back_cos[..., 0], back_sin[..., 0], back_cos[..., 1], back_sin[..., 1]], axis=-1
    )
    return returned.astype(jnp.bfloat16).reshape(orders_total, cycles_here, columns)


def analyse(order_fields, table_rows, vectors):
    orders_here, cycles_here, columns = order_fields.shape
    pieces = order_fields.reshape(orders_here, cycles_here, vectors, 4)
    adjoint = adjoint_terms(pieces).reshape(orders_here, 2, cycles_here, columns)
    applied = lax.dot_general(
        adjoint, table_rows, (((1, 2), (1, 2)), ((0,), (0,))), preferred_element_type=jnp.float32
    )
    applied = applied.reshape(orders_here, vectors, 4, table_rows.shape[3])
    return applied.transpose(1, 0, 2, 3).astype(jnp.bfloat16)


def gram_terms(trial_part, applied_part):
    trial_flat = trial_part.reshape(trial_part.shape[0], -1)
    applied_flat = applied_part.reshape(applied_part.shape[0], -1)
    dims = (((1,), (1,)), ((), ()))
    gram_trial = lax.dot_general(trial_flat, trial_flat, dims, preferred_element_type=jnp.float32)
    cross = lax.dot_general(trial_flat, applied_flat, dims, preferred_element_type=jnp.float32)
    gram_applied = lax.dot_general(
        applied_flat, applied_flat, dims, preferred_element_type=jnp.float32
    )
    return (gram_trial, cross, gram_applied)


def finish_ritz(totals, coefficients):
    gram_trial = totals[0] / coefficients
    cross = totals[1] / coefficients
    gram_applied = totals[2] / coefficients
    factor_trial = jnp.linalg.cholesky(gram_trial)
    half_solved = lax.linalg.triangular_solve(factor_trial, cross, left_side=True, lower=True)
    ritz_matrix = lax.linalg.triangular_solve(
        factor_trial, half_solved.T, left_side=True, lower=True
    ).T
    factor_applied = jnp.linalg.cholesky(gram_applied)
    identity = jnp.eye(gram_applied.shape[0], dtype=jnp.float32)
    mixing = lax.linalg.triangular_solve(factor_applied, identity, left_side=True, lower=True)
    return (ritz_matrix, mixing.astype(jnp.bfloat16))


def shards(trial_block, legendre, order_slot, cycle_start, cycle_count, cycle_weight):
    vectors = trial_block.shape[0]
    orders_here = trial_block.shape[1]
    degrees = trial_block.shape[3]
    fields = synthesize(trial_block, legendre)
    cycle_fields = lax.all_to_all(fields, "ma", split_axis=1, concat_axis=0, tiled=True)
    per_device = cycle_fields.shape[1]
    cycle_first = lax.axis_index("ma") * per_device
    returned = cycle_transform(
        cycle_fields, cycle_first, order_slot, cycle_start, cycle_count, cycle_weight
    )
    order_fields = lax.all_to_all(returned, "ma", split_axis=0, concat_axis=1, tiled=True)
    applied = analyse(order_fields, legendre, vectors)
    coefficients = lax.axis_size("ma") * orders_here * 4 * degrees
    trial_all, applied_all = (
        lax.all_gather(trial_block, "vert", axis=0, tiled=True),
        lax.all_gather(applied, "vert", axis=0, tiled=True),
    )
    totals = lax.psum(gram_terms(trial_all, applied_all), "ma")
    ritz_matrix, mixing = finish_ritz(totals, coefficients)
    mix_rows = lax.dynamic_slice_in_dim(mixing, lax.axis_index("vert") * vectors, vectors, 0)
    mixed = jnp.dot(
        mix_rows, applied_all.reshape(applied_all.shape[0], -1), preferred_element_type=jnp.float32
    )
    new_basis = mixed.reshape(trial_block.shape).astype(jnp.bfloat16)
    return (new_basis, ritz_matrix)


def solution(mesh):
    in_specs = (P("vert", "ma", None, None), P("ma", None, None, None), P(), P(), P(), P())
    out_specs = (P("vert", "ma", None, None), P())
    return jax.shard_map(shards, mesh=mesh, in_specs=in_specs, out_specs=out_specs, check_vma=False)
```

profile of v0, /device:TPU:0, one launch (start us, length us, event | category | flops | bytes accessed | tf_op | source)
XLA Modules:
  0.0 283.7 jit_solution(16547234983616233093)
XLA Ops:
  7.2 0.0 all-gather.5.cloned.1.call-start
  7.2 4.2 %copy.113 = bf16[32,8,4,1024]{3,0,2,1:T(8,128)(2,1)} copy(bf16[32,8,4,1024]{3,2,1,0:T(4,128)(2,1)} %param.9) | data formatting | bytes 4194304 | tf_op args[0]
  11.4 1.6 copy-done.2
  13.0 1.9 fusion.2
  14.9 0.1 slice_bitcast_fusion
  14.9 0.1 fusion.16
  15.1 0.1 pad_maximum_fusion.2
  15.1 0.4 copy.96
  15.6 0.8 copy.97
  16.4 7.3 %all-to-all-start = ((bf16[8,32,128]{2,0,1:T(8,128)(2,1)}), bf16[8,32,128]{2,0,1:T(8,128)(2,1)S(1)}, u32[]{:S(2)}, u32[]{:S(2)}) async-start(bf16[8,32,128]{2,0,1:T(8,128)(2,1)} %copy.97), calls=%async_computation | async-start | bytes 131072 | tf_op jit(solution)/shard_map/all_to_all | solution.py:126
  23.7 0.0 all-gather.3.cloned.1.call-start
  23.8 0.1 dynamic_slice.12
  23.9 0.1 dynamic_slice.13
  23.9 0.1 dynamic_slice.14
  24.0 0.1 fusion.51
  24.1 6.5 %all-to-all-done = bf16[8,32,128]{2,0,1:T(8,128)(2,1)S(1)} async-done(((bf16[8,32,128]{2,0,1:T(8,128)(2,1)}), bf16[8,32,128]{2,0,1:T(8,128)(2,1)S(1)}, u32[]{:S(2)}, u32[]{:S(2)}) %all-to-all-start) | async-done | bytes 65568 | tf_op jit(solution)/shard_map/all_to_all | solution.py:126
  30.6 0.5 copy.98
  31.1 0.7 reshape.96
  31.8 0.3 slice.83
  32.2 0.3 slice.84
  32.5 0.3 fusion.23
  32.8 0.3 fusion.9
  33.2 0.3 fusion.10
  33.5 0.3 fusion.11
  33.9 0.1 copy.101
  34.0 0.1 copy.102
  34.1 9.3 %all_to_all.30 = bf16[64,4,128]{2,1,0:T(4,128)(2,1)S(1)} all-to-all(bf16[64,4,128]{2,1,0:T(4,128)(2,1)S(1)} %copy.102), channel_id=1, replica_groups=mesh['ma'=8,'vert'=4] {'ma'}, dimensions={0} | all-to-all | bytes 131072 | tf_op jit(solution)/shard_map/all_to_all | solution.py:132
  43.4 0.5 copy.104
  43.9 0.4 slice.108
  44.4 2.7 slice_negate_fusion.3
  47.1 5.2 %pad_maximum_fusion = (bf16[8,32,32,4]{0,3,2,1:T(4,128)(2,1)S(1)}, bf16[8,32,32,4]{0,3,2,1:T(4,128)(2,1)S(1)}) fusion(bf16[8,32,32,1]{0,3,2,1:T(2,128)(2,1)S(1)} %get-tuple-element.20, bf16[8,32,32,1]{0,3,2,1:T(2,128)(2,1)S(1)} %get-tuple-element.17, bf16[8,32,32,2]{0,3,2,1:T(2,128)(2,1)S(1)} %slice.108, bf16[8,32,32,1]{0,3,2,1:T(2,128)(2,1)S(1)} %get-tuple-element.18, ...), kind=kLoop, calls=%fused_computation.20 | loop fusion | flops 458752 | bytes 245760 | tf_op jit(solution)/shard_map/stack | solution.py:28
  52.3 0.4 copy.107
  52.6 0.4 copy.108
  53.0 0.7 bitcast_convert_fusion
  53.7 2.2 convert_element_type.52
  55.9 3.6 %copy.146 = bf16[8,32,4,1024]{3,1,2,0:T(8,128)(2,1)} copy(bf16[8,32,4,1024]{3,2,1,0:T(4,128)(2,1)} %convert_element_type.52) | data formatting | bytes 4194304 | tf_op jit(solution)/shard_map/convert_element_type | solution.py:91
  59.6 0.3 all-reduce.3.cloned.1.call-start
  59.8 12.7 %all-gather.5.cloned.1.call-done = bf16[128,8,4,1024]{3,0,2,1:T(8,128)(2,1)} async-done(((bf16[32,8,4,1024]{3,0,2,1:T(8,128)(2,1)}), bf16[128,8,4,1024]{3,0,2,1:T(8,128)(2,1)}) %all-gather.5.cloned.1.call-update) | async-done | bytes 8388624 | tf_op jit(solution)/shard_map/all_gather | solution.py:136
  72.6 8.7 %convolution_bitcast_fusion.3 = f32[128,128]{0,1:T(8,128)} fusion(bf16[128,8,4,1024]{3,0,2,1:T(8,128)(2,1)} %all-gather.5.cloned.1.call-done), kind=kOutput, calls=%fused_computation.18 | convolution fusion | flops 1073741824 | bytes 8454144 | tf_op jit(solution)/shard_map/dot_general | solution.py:98
  81.3 51.2 %all-gather.3.cloned.1.call-done = bf16[128,8,4,1024]{3,0,2,1:T(8,128)(2,1)} async-done(((bf16[32,8,4,1024]{3,0,2,1:T(8,128)(2,1)}), bf16[128,8,4,1024]{3,0,2,1:T(8,128)(2,1)}) %all-gather.3.cloned.1.call-update) | async-done | bytes 8388624 | tf_op jit(solution)/shard_map/all_gather | solution.py:137
  132.5 8.9 %convolution_bitcast_fusion.2 = f32[128,128]{0,1:T(8,128)} fusion(bf16[128,8,4,1024]{3,0,2,1:T(8,128)(2,1)} %all-gather.3.cloned.1.call-done, bf16[128,8,4,1024]{3,0,2,1:T(8,128)(2,1)} %all-gather.5.cloned.1.call-done), kind=kOutput, calls=%fused_computation.17 | convolution fusion | flops 1073741824 | bytes 16842752 | tf_op jit(solution)/shard_map/dot_general | solution.py:99
  141.3 3.0 %convolution_bitcast_fusion.4 = f32[128,128]{0,1:T(8,128)} fusion(bf16[128,8,4,1024]{3,0,2,1:T(8,128)(2,1)S(1)} %copy-done.1), kind=kOutput, calls=%fused_computation.19 | convolution fusion | flops 1073741824 | bytes 8454144 | tf_op jit(solution)/shard_map/dot_general | solution.py:100
  144.3 11.5 %copy.112 = bf16[128,8,4,1024]{0,3,2,1:T(8,128)(2,1)} copy(bf16[128,8,4,1024]{3,0,2,1:T(8,128)(2,1)} %all-gather.3.cloned.1.call-done) | data formatting | bytes 16777216 | tf_op jit(solution)/shard_map/all_gather | solution.py:137
  155.8 60.1 %all-reduce.3.cloned.1.call-done = (f32[128,128]{0,1:T(8,128)}, f32[128,128]{0,1:T(8,128)}, f32[128,128]{0,1:T(8,128)}) async-done(((f32[128,128]{0,1:T(8,128)}, f32[128,128]{0,1:T(8,128)}, f32[128,128]{0,1:T(8,128)}), (f32[128,128]{0,1:T(8,128)}, f32[128,128]{0,1:T(8,128)}, f32[128,128]{0,1:T(8,128)})) %all-reduce.3.cloned.1.call-update) | async-done | bytes 196624 | tf_op jit(solution)/shard_map/psum | solution.py:139
  215.8 0.8 broadcast_multiply_fusion
  216.7 0.1 copy.115
  216.8 0.9 fusion.27
  217.6 11.7 %cholesky.55 = f32[128,128]{1,0:T(8,128)S(1)} custom-call(f32[128,128]{1,0:T(8,128)S(1)} %fusion.27), custom_call_target="Cholesky" | custom-call | tf_op jit(solution)/shard_map/jit(cholesky)/cholesky | solution.py:110
  229.4 0.6 compare_reduce_fusion
  230.0 0.7 fusion.21
  230.7 9.8 %custom-call.9 = f32[1,128,128]{1,2,0:T(8,128)S(1)} custom-call(f32[1,128,128]{2,1,0:T(8,128)S(1)} %fusion.21), custom_call_target="InvertDiagBlocksLowerTriangular" | custom-call | tf_op jit(solution)/shard_map/triangular_solve/custom-call.0 | solution.py:112
  240.5 1.1 convolution_bitcast_fusion.1
  241.6 0.3 convolution_bitcast_fusion
  241.9 0.7 copy.117
  242.7 0.8 broadcast_multiply_fusion.1
  243.5 0.1 copy.111
  243.6 0.9 fusion.30
  244.5 11.7 %cholesky.44 = f32[128,128]{1,0:T(8,128)S(1)} custom-call(f32[128,128]{1,0:T(8,128)S(1)} %fusion.30), custom_call_target="Cholesky" | custom-call | tf_op jit(solution)/shard_map/jit(cholesky)/cholesky | solution.py:115
  256.2 0.6 compare_reduce_fusion.1
  256.9 0.7 fusion.20
  257.5 10.1 %custom-call.7 = f32[1,128,128]{1,2,0:T(8,128)S(1)} custom-call(f32[1,128,128]{2,1,0:T(8,128)S(1)} %fusion.20), custom_call_target="InvertDiagBlocksLowerTriangular" | custom-call | tf_op jit(solution)/shard_map/triangular_solve/custom-call.0 | solution.py:117
  267.6 0.3 fusion.28
  267.9 6.4 %fusion.4 = bf16[32,8,4,1024]{3,0,2,1:T(8,128)(2,1)S(1)} fusion(bf16[128,8,4,1024]{0,3,2,1:T(8,128)(2,1)} %copy.112, bf16[128,128]{1,0:T(8,128)(2,1)S(1)} %fusion.28, s32[]{:T(128)S(6)} %select_n.31), kind=kOutput, calls=%fused_computation.6 | convolution fusion | flops 269484032 | bytes 10493956 | tf_op jit(solution)/shard_map/dot_general | solution.py:142
  274.3 2.9 %copy.116 = bf16[32,8,4,1024]{3,2,1,0:T(4,128)(2,1)} copy(bf16[32,8,4,1024]{3,0,2,1:T(8,128)(2,1)S(1)} %fusion.4) | data formatting | bytes 4194304
  (21 shorter events, 0.2 us)
Async XLA Ops:
  7.2 4.2 %copy-start = (bf16[8,2,32,1024]{3,2,1,0:T(8,128)(2,1)S(1)}, bf16[8,2,32,1024]{3,2,1,0:T(8,128)(2,1)}, u32[]{:S(2)}) copy-start(bf16[8,2,32,1024]{3,2,1,0:T(8,128)(2,1)} %param.10) | copy-start | bytes 3145732
  7.2 65.4 %all-gather.5.cloned.1.call-start = ((), (), s32[]{:S(2)}) async-start(), calls=%async_computation.3 | async-start | bytes 10485760 | tf_op jit(solution)/shard_map/all_gather | solution.py:136
  11.4 1.6 copy-start.2
  14.8 8.9 %copy-start.3 = (s32[32]{0:T(128)S(1)}, s32[32]{0:T(128)}, u32[]{:S(2)}) copy-start(s32[32]{0:T(128)} %param.12) | copy-start | bytes 388
  14.8 9.0 %copy-start.4 = (s32[32]{0:T(128)S(1)}, s32[32]{0:T(128)}, u32[]{:S(2)}) copy-start(s32[32]{0:T(128)} %param.13) | copy-start | bytes 388
  14.9 9.1 %copy-start.5 = (f32[32]{0:T(128)S(1)}, f32[32]{0:T(128)}, u32[]{:S(2)}) copy-start(f32[32]{0:T(128)} %param.14) | copy-start | bytes 388
  15.0 17.4 %copy-start.6 = (s32[64]{0:T(128)S(1)}, s32[64]{0:T(128)}, u32[]{:S(2)}) copy-start(s32[64]{0:T(128)} %param.11) | copy-start | bytes 772
  16.4 14.2 %all-to-all-start = ((bf16[8,32,128]{2,0,1:T(8,128)(2,1)}), bf16[8,32,128]{2,0,1:T(8,128)(2,1)S(1)}, u32[]{:S(2)}, u32[]{:S(2)}) async-start(bf16[8,32,128]{2,0,1:T(8,128)(2,1)} %copy.97), calls=%async_computation | async-start | bytes 131072 | tf_op jit(solution)/shard_map/all_to_all | solution.py:126
  23.7 108.7 %all-gather.3.cloned.1.call-start = ((), (), s32[]{:S(2)}) async-start(), calls=%async_computation.2 | async-start | bytes 10485760 | tf_op jit(solution)/shard_map/all_gather | solution.py:137
  59.6 156.3 %all-reduce.3.cloned.1.call-start = ((), (), s32[]{:S(2)}) async-start(), calls=%async_computation.4 | async-start | bytes 393216 | tf_op jit(solution)/shard_map/psum | solution.py:139
  132.4 8.9 %copy-start.1 = (bf16[128,8,4,1024]{3,0,2,1:T(8,128)(2,1)S(1)}, bf16[128,8,4,1024]{3,0,2,1:T(8,128)(2,1)}, u32[]{:S(2)}) copy-start(bf16[128,8,4,1024]{3,0,2,1:T(8,128)(2,1)} %all-gather.3.cloned.1.call-done) | copy-start | bytes 25165828
Sparse Core Ops, SparseCore 0:
  11.5 60.9 all-gather.4
  74.1 58.2 all-gather.2
  144.4 71.3 all-reduce.2
where the time goes:
time: 285 us; the launch traced here: 284 us
  waiting for transfers between devices  131 us (46%)
  other arithmetic  57.5 us (20%)
  matrix products  32.5 us (11%)
  local copies, waits for them, and re-layouts  32.1 us (11%)
  between operations  14.1 us (5%)
  blocking collectives  9.29 us (3%)
  starting transfers between devices  7.65 us (3%)
    psum x1, waiting for transfers between devices, shards(): totals = lax.psum(gram_terms(trial_all, applied_all), 'ma')  60.1 us
    all_gather x1, waiting for transfers between devices, shards(): lax.all_gather(applied, 'vert', axis=0, tiled=True)  51.2 us
    all_gather x1, waiting for transfers between devices, shards(): lax.all_gather(trial_block, 'vert', axis=0, tiled=True)  12.7 us
    another operation x3, other arithmetic, finish_ritz(): factor_applied = jnp.linalg.cholesky(gram_applied)  12.4 us
    another operation x3, other arithmetic, finish_ritz(): factor_trial = jnp.linalg.cholesky(gram_trial)  12.4 us
    all_gather x1, local copies, waits for them, and re-layouts, shards(): lax.all_gather(applied, 'vert', axis=0, tiled=True)  11.5 us
    another operation x2, other arithmetic, finish_ritz(): lax.linalg.triangular_solve(factor_applied, identity, left_side=True, low...  10.7 us
    another operation x2, other arithmetic, finish_ritz(): lax.linalg.triangular_solve(factor_trial, half_solved.T, left_side=True,...  10.5 us
  transfers between devices with their start and end apart: 4, of which 4 were waited for; matrix products, arithmetic and copies ran while one was open for 15% of the time, Pallas kernels for 0%

commit v1 on v0

v1 whole, which is shorter than its diff:
```python
import functools
import math

import jax
import jax.numpy as jnp
from jax import lax
from jax.experimental import pallas as pl
from jax.experimental.pallas import tpu as pltpu
from jax.sharding import PartitionSpec as P

MESH = pl.DeviceIdType.MESH
VMEM = pltpu.VMEM
F32 = jnp.float32
BF16 = jnp.bfloat16
HIGHEST = lax.Precision.HIGHEST
GRANT = 60 * 1024 * 1024


def on_vmem(count):
    return [pl.BlockSpec(memory_space=VMEM)] * count


def transform_kernel(
    n_ma, n_vert, width, own_ref, table_ref, back_ref, factor_ref, out_ref,
    gathered, ma_send, ma_recv, vert_send, vert_recv,
):
    ma = lax.axis_index("ma")
    vert = lax.axis_index("vert")
    rows = own_ref.shape[0]
    columns = own_ref.shape[1]
    barrier = pltpu.get_barrier_semaphore()

    def greet_ma(step, carry):
        pl.semaphore_signal(
            barrier, inc=1, device_id=(lax.rem(ma + step, n_ma), vert), device_id_type=MESH
        )
        return carry

    def greet_vert(step, carry):
        pl.semaphore_signal(
            barrier, inc=1, device_id=(ma, lax.rem(vert + step, n_vert)), device_id_type=MESH
        )
        return carry

    lax.fori_loop(1, n_ma, greet_ma, 0)
    lax.fori_loop(1, n_vert, greet_vert, 0)
    pl.semaphore_wait(barrier, n_ma + n_vert - 2)

    def ma_copy(slot, peer):
        return pltpu.make_async_remote_copy(
            src_ref=own_ref,
            dst_ref=gathered.at[slot],
            send_sem=ma_send.at[peer],
            recv_sem=ma_recv.at[slot],
            device_id=(peer, vert),
            device_id_type=MESH,
        )

    def start_ma(step, carry):
        ma_copy(ma, lax.rem(ma + step, n_ma)).start()
        return carry

    def wait_ma(step, carry):
        other = lax.rem(ma + step, n_ma)
        ma_copy(ma, other).wait_send()
        ma_copy(other, other).wait_recv()
        return carry

    lax.fori_loop(1, n_ma, start_ma, 0)
    gathered[ma] = own_ref[...]
    lax.fori_loop(1, n_ma, wait_ma, 0)

    def column_block(block, carry):
        at = pl.ds(pl.multiple_of(block * width, width), width)
        fields = gathered[:, :, at].reshape(n_ma * rows, width)
        grid = jnp.dot(table_ref[...], fields, preferred_element_type=F32)
        weighted = (grid * factor_ref[:, at]).astype(BF16)
        back = jnp.dot(back_ref[...], weighted, preferred_element_type=F32)
        out_ref[vert, :, at] = back.astype(BF16)
        return carry

    lax.fori_loop(0, columns // width, column_block, 0)

    def vert_copy(slot, peer):
        return pltpu.make_async_remote_copy(
            src_ref=out_ref.at[slot],
            dst_ref=out_ref.at[slot],
            send_sem=vert_send.at[peer],
            recv_sem=vert_recv.at[slot],
            device_id=(ma, peer),
            device_id_type=MESH,
        )

    def start_vert(step, carry):
        vert_copy(vert, lax.rem(vert + step, n_vert)).start()
        return carry

    def wait_vert(step, carry):
        other = lax.rem(vert + step, n_vert)
        vert_copy(vert, other).wait_send()
        vert_copy(other, other).wait_recv()
        return carry

    lax.fori_loop(1, n_vert, start_vert, 0)
    lax.fori_loop(1, n_vert, wait_vert, 0)


def transform(own, table, back, factor, n_ma, n_vert):
    rows, columns = own.shape
    return pl.pallas_call(
        functools.partial(transform_kernel, n_ma, n_vert, min(columns, 512)),
        out_shape=jax.ShapeDtypeStruct((n_vert, rows, columns), BF16),
        in_specs=on_vmem(4),
        out_specs=pl.BlockSpec(memory_space=VMEM),
        scratch_shapes=[
            VMEM((n_ma, rows, columns), BF16),
            pltpu.SemaphoreType.DMA((n_ma,)),
            pltpu.SemaphoreType.DMA((n_ma,)),
            pltpu.SemaphoreType.DMA((n_vert,)),
            pltpu.SemaphoreType.DMA((n_vert,)),
        ],
        compiler_params=pltpu.CompilerParams(
            collective_id=0, has_side_effects=True, vmem_limit_bytes=GRANT
        ),
        name="transform",
    )(own, table, back, factor)


def applied_kernel(g_ref, table_ref, out_ref):
    table = table_ref[0]
    g = [g_ref[0, part].astype(F32) for part in range(4)]
    pairs = [(g[0], -g[3]), (g[1], g[2]), (-g[2], -g[1]), (-g[3], g[0])]
    for part, (first, second) in enumerate(pairs):
        adjoint = jnp.concatenate([first, second], axis=0).astype(BF16)
        out = lax.dot_general(
            adjoint, table, (((0,), (0,)), ((), ())), preferred_element_type=F32
        )
        out_ref[0, part] = out.astype(BF16)


def apply_tables(g, table):
    orders, parts, cycles, vectors = g.shape
    depth, degrees = table.shape[1:]
    return pl.pallas_call(
        applied_kernel,
        grid=(orders,),
        out_shape=jax.ShapeDtypeStruct((orders, parts, vectors, degrees), BF16),
        in_specs=[
            pl.BlockSpec((1, parts, cycles, vectors), lambda s: (s, 0, 0, 0)),
            pl.BlockSpec((1, depth, degrees), lambda s: (s, 0, 0)),
        ],
        out_specs=pl.BlockSpec((1, parts, vectors, degrees), lambda s: (s, 0, 0, 0)),
        compiler_params=pltpu.CompilerParams(vmem_limit_bytes=32 * 1024 * 1024),
        cost_estimate=pl.CostEstimate(
            flops=16 * orders * parts * vectors * degrees * depth,
            bytes_accessed=orders * parts * vectors * degrees * 2,
            transcendentals=0,
        ),
        name="apply_tables",
    )(g, table)


def gram_kernel(n_vert, at_ref, *refs):
    pieces = refs[:n_vert]
    applied_ref, out_ref, trial = refs[n_vert], refs[n_vert + 1], refs[n_vert + 2]
    vert = at_ref[0]
    vectors = pieces[0].shape[3 - 1]
    first = (pl.program_id(0) == 0) & (pl.program_id(1) == 0)
    for step in range(n_vert):
        place = lax.rem(vert + step, n_vert)
        trial[pl.ds(pl.multiple_of(place * vectors, vectors), vectors), :] = pieces[step][0, 0]

    @pl.when(first)
    def _():
        out_ref[...] = jnp.zeros_like(out_ref)

    dims = (((1,), (1,)), ((), ()))
    t = trial[...]
    a = applied_ref[0, 0]
    out_ref[0] += lax.dot_general(t, t, dims, preferred_element_type=F32)
    out_ref[1] += lax.dot_general(t, a, dims, preferred_element_type=F32)
    out_ref[2] += lax.dot_general(a, a, dims, preferred_element_type=F32)


def gram_terms(at, own, received, applied, n_vert):
    orders, parts, vectors, degrees = own.shape
    share = orders // n_vert
    total = n_vert * vectors
    block = (1, 1, vectors, degrees)
    flops = 12 * share * parts * total * total * degrees
    return pl.pallas_call(
        functools.partial(gram_kernel, n_vert),
        grid_spec=pltpu.PrefetchScalarGridSpec(
            num_scalar_prefetch=1,
            grid=(share, parts),
            in_specs=[pl.BlockSpec(block, lambda s, c, at: (at[0] * share + s, c, 0, 0))]
            + [pl.BlockSpec(block, lambda s, c, at: (s, c, 0, 0))] * (n_vert - 1)
            + [
                pl.BlockSpec(
                    (1, 1, total, degrees), lambda s, c, at: (at[0] * share + s, c, 0, 0)
                )
            ],
            out_specs=pl.BlockSpec((3, total, total), lambda s, c, at: (0, 0, 0)),
            scratch_shapes=[VMEM((total, degrees), BF16)],
        ),
        out_shape=jax.ShapeDtypeStruct((3, total, total), F32),
        compiler_params=pltpu.CompilerParams(vmem_limit_bytes=32 * 1024 * 1024),
        cost_estimate=pl.CostEstimate(
            flops=flops, bytes_accessed=4 * share * parts * total * degrees, transcendentals=0
        ),
        name="gram_terms",
    )(at, own, *received, applied)


def sum_kernel(n_vert, count, part_ref, out_ref, landed, send_a, recv_a, send_b, recv_b):
    me = lax.axis_index("ma") * n_vert + lax.axis_index("vert")
    barrier = pltpu.get_barrier_semaphore()

    def where(flat):
        return (flat // n_vert, lax.rem(flat, n_vert))

    def greet(step, carry):
        other = lax.rem(me + step, count)
        pl.semaphore_signal(barrier, inc=1, device_id=where(other), device_id_type=MESH)
        return carry

    lax.fori_loop(1, count, greet, 0)
    pl.semaphore_wait(barrier, count - 1)

    def scatter(peer, slot):
        return pltpu.make_async_remote_copy(
            src_ref=part_ref.at[peer],
            dst_ref=landed.at[slot],
            send_sem=send_a.at[peer],
            recv_sem=recv_a.at[slot],
            device_id=where(peer),
            device_id_type=MESH,
        )

    def gather(peer, slot):
        return pltpu.make_async_remote_copy(
            src_ref=out_ref.at[slot],
            dst_ref=out_ref.at[slot],
            send_sem=send_b.at[peer],
            recv_sem=recv_b.at[slot],
            device_id=where(peer),
            device_id_type=MESH,
        )

    def exchange(copy):
        def start(step, carry):
            copy(lax.rem(me + step, count), me).start()
            return carry

        def wait(step, carry):
            other = lax.rem(me + step, count)
            copy(other, me).wait_send()
            copy(other, other).wait_recv()
            return carry

        return start, wait

    start, wait = exchange(scatter)
    lax.fori_loop(1, count, start, 0)
    landed[me] = part_ref[me]
    lax.fori_loop(1, count, wait, 0)
    out_ref[me] = jnp.sum(landed[...], axis=0)
    start, wait = exchange(gather)
    lax.fori_loop(1, count, start, 0)
    lax.fori_loop(1, count, wait, 0)


def sum_over_devices(terms, n_ma, n_vert):
    count = n_ma * n_vert
    lanes = terms.shape[-1]
    rows = terms.size // lanes
    each = -(-rows // count)
    flat = terms.reshape(rows, lanes)
    if each * count != rows:
        flat = jnp.pad(flat, ((0, each * count - rows), (0, 0)))
    slots = flat.reshape(count, each, lanes)
    out = pl.pallas_call(
        functools.partial(sum_kernel, n_vert, count),
        out_shape=jax.ShapeDtypeStruct(slots.shape, F32),
        in_specs=on_vmem(1),
        out_specs=pl.BlockSpec(memory_space=VMEM),
        scratch_shapes=[VMEM(slots.shape, F32)] + [pltpu.SemaphoreType.DMA((count,))] * 4,
        compiler_params=pltpu.CompilerParams(collective_id=1, has_side_effects=True),
        name="sum_over_devices",
    )(slots)
    return out.reshape(each * count, lanes)[:rows].reshape(terms.shape)


def factor_kernel(coefficients, totals_ref, ritz_ref, mixing_ref, work):
    size = ritz_ref.shape[0]
    panel = 8
    scale = 1.0 / coefficients
    row_at = lax.broadcasted_iota(jnp.int32, (size, size), 0)
    column_at = lax.broadcasted_iota(jnp.int32, (size, size), 1)
    identity = (row_at == column_at).astype(F32)
    for b, source in enumerate((0, 2)):
        work[b, :, :size] = totals_ref[source] * scale
        work[b, :, size:] = identity
    lane = lax.broadcasted_iota(jnp.int32, (panel, size), 1)
    sub = lax.broadcasted_iota(jnp.int32, (panel, 2 * size), 0)
    all_rows = lax.broadcasted_iota(jnp.int32, (size, 2 * size), 0)

    def panel_step(p, carry):
        first = pl.multiple_of(p * panel, panel)
        at = pl.ds(first, panel)
        panels = [work[b, at, :] for b in range(2)]
        for i in range(panel):
            for b in range(2):
                x = panels[b]
                column = jnp.sum(
                    jnp.where(lane == first + i, x[:, :size], 0.0), axis=1, keepdims=True
                )
                inverse = lax.rsqrt(column[i : i + 1, :])
                line = x[i : i + 1, :] * inverse
                lower = x - (column * inverse) * line
                panels[b] = jnp.where(sub == i, line, jnp.where(sub > i, lower, x))
        for b in range(2):
            x = panels[b]
            update = lax.dot_general(
                x[:, :size], x, (((0,), (0,)), ((), ())),
                precision=HIGHEST, preferred_element_type=F32,
            )
            below = all_rows >= first + panel
            work[b] = jnp.where(below, work[b] - update, work[b])
            work[b, at, :] = x
        return carry

    lax.fori_loop(0, size // panel, panel_step, 0)
    inverse_trial = work[0, :, size:]
    half = jnp.dot(
        inverse_trial, totals_ref[1] * scale, precision=HIGHEST, preferred_element_type=F32
    )
    ritz_ref[...] = lax.dot_general(
        half, inverse_trial, (((1,), (1,)), ((), ())),
        precision=HIGHEST, preferred_element_type=F32,
    )
    mixing_ref[...] = work[1, :, size:].astype(BF16)


def finish_ritz(totals, coefficients):
    size = totals.shape[-1]
    return pl.pallas_call(
        functools.partial(factor_kernel, float(coefficients)),
        out_shape=(
            jax.ShapeDtypeStruct((size, size), F32),
            jax.ShapeDtypeStruct((size, size), BF16),
        ),
        in_specs=on_vmem(1),
        out_specs=(pl.BlockSpec(memory_space=VMEM), pl.BlockSpec(memory_space=VMEM)),
        scratch_shapes=[VMEM((2, size, 2 * size), F32)],
        name="finish_ritz",
    )(totals)


def fourier_tables(order_slot, longitudes, orders_total):
    longitude = jnp.arange(longitudes, dtype=jnp.int32)
    phases = longitude[:, None] * order_slot[None, :] % longitudes
    angles = phases.astype(F32) * (2.0 * math.pi / longitudes)
    scale = 1.0 / math.sqrt(orders_total)
    return ((jnp.cos(angles) * scale).astype(BF16), (jnp.sin(angles) * scale).astype(BF16))


def shards(trial_block, legendre, order_slot, cycle_start, cycle_count, cycle_weight):
    n_ma = lax.axis_size("ma")
    n_vert = lax.axis_size("vert")
    ma = lax.axis_index("ma")
    vert = lax.axis_index("vert")
    vectors, orders, parts, degrees = trial_block.shape
    orders_total = order_slot.shape[0]
    cycles = cycle_count.shape[0]
    live = cycles // 4
    longitudes = 2 * orders_total

    first = jnp.minimum(jnp.argmax(cycle_count > 0), cycles - live).astype(jnp.int32)
    table = lax.dynamic_slice_in_dim(legendre, first, live, 2).reshape(orders, 2 * live, degrees)
    trial = trial_block.transpose(1, 2, 0, 3)

    share = orders // n_vert
    received = []
    for step in range(1, n_vert):
        ring = [(source, (source - step) % n_vert) for source in range(n_vert)]
        target = (vert - step) % n_vert
        piece = lax.dynamic_slice_in_dim(trial, target * share, share, 0)
        received.append(lax.ppermute(piece, "vert", ring))

    products = lax.dot_general(
        table, trial, (((2,), (3,)), ((0,), (0,))), preferred_element_type=F32
    )
    w = products[:, :live]
    x = products[:, live:]
    cosine_parts = jnp.stack([w[:, :, 0] + x[:, :, 3], x[:, :, 1] - w[:, :, 2]], axis=2)
    sine_parts = jnp.stack([w[:, :, 1] - x[:, :, 2], -x[:, :, 0] - w[:, :, 3]], axis=2)
    own = jnp.stack([cosine_parts, sine_parts], axis=0).astype(BF16)
    own = own.reshape(2 * orders, live * 2 * vectors)

    cosine, sines = fourier_tables(order_slot, longitudes, orders_total)
    tables = jnp.stack(
        [
            cosine.reshape(longitudes, n_ma, orders),
            sines.reshape(longitudes, n_ma, orders),
        ],
        axis=2,
    )
    back = lax.dynamic_index_in_dim(tables, ma, 1, keepdims=False)
    back = back.reshape(longitudes, 2 * orders).T
    tables = tables.reshape(longitudes, n_ma * 2 * orders)
    starts = lax.dynamic_slice_in_dim(cycle_start, first, live)
    counts = lax.dynamic_slice_in_dim(cycle_count, first, live)
    weights = lax.dynamic_slice_in_dim(cycle_weight, first, live)
    longitude = jnp.arange(longitudes, dtype=jnp.int32)
    inside = (longitude[:, None] - starts[None, :]) % longitudes < counts[None, :]
    factor = inside.astype(F32) * weights[None, :]
    factor = jnp.broadcast_to(factor[:, :, None], (longitudes, live, 2 * vectors))
    factor = factor.reshape(longitudes, live * 2 * vectors)

    returned = transform(own, tables, back, factor, n_ma, n_vert)
    g = returned.reshape(n_vert, 2, orders, live, 2, vectors).transpose(2, 4, 1, 3, 0, 5)
    g = g.reshape(orders, 4, live, n_vert * vectors)
    applied = apply_tables(g, table)

    terms = gram_terms(vert[None].astype(jnp.int32), trial, received, applied, n_vert)
    totals = sum_over_devices(terms, n_ma, n_vert)
    ritz_matrix, mixing = finish_ritz(totals, orders_total * parts * degrees)
    mix_rows = lax.dynamic_slice_in_dim(mixing, vert * vectors, vectors, 0)
    mixed = jnp.einsum("km,scml->kscl", mix_rows, applied, preferred_element_type=F32)
    return (mixed.astype(BF16), ritz_matrix)


def solution(mesh):
    in_specs = (P("vert", "ma", None, None), P("ma", None, None, None), P(), P(), P(), P())
    out_specs = (P("vert", "ma", None, None), P())
    return jax.shard_map(shards, mesh=mesh, in_specs=in_specs, out_specs=out_specs, check_vma=False)
```

time: 285 us -> 99.9 us (0.35)
  waiting for transfers between devices: 131 us -> 0.01 us
  Pallas kernels: 0 us -> 65.4 us
  other arithmetic: 57.5 us -> 1.71 us
  matrix products: 32.5 us -> 7.7 us
  local copies, waits for them, and re-layouts: 32.1 us -> 18.4 us
  between operations: 14.1 us -> 1.61 us
  blocking collectives: 9.29 us -> 0 us
  starting transfers between devices: 7.65 us -> 4.43 us
    pallas_call x0 -> x5, Pallas kernels: none -> 65.4 us  [the longest x1 21 us: sum_over_devices(): pl.pallas_call(functools.partial(sum_kernel, n_vert, count), out_shape=ja...]
    all_gather x2 -> x0, waiting for transfers between devices: 63.9 us -> none  [the longest x1 51.2 us: shards(): lax.all_gather(applied, 'vert', axis=0, tiled=True)]
    psum x1 -> x0, waiting for transfers between devices: 60.1 us -> none  [shards(): totals = lax.psum(gram_terms(trial_all, applied_all), 'ma')]
    another operation x14 -> x5, other arithmetic: 51.4 us -> 0.81 us  [the longest x1 0.73 us: shards(): jnp.argmax(cycle_count > 0)]
    dot_general x10 -> x2, matrix products: 30.9 us -> 7.7 us  [the longest x1 4.62 us: shards(): jnp.einsum('km,scml->kscl', mix_rows, applied, preferred_element_type=F32)]
    all_gather x1 -> x0, local copies, waits for them, and re-layouts: 11.5 us -> none  [shards(): lax.all_gather(applied, 'vert', axis=0, tiled=True)]
    all_to_all x1 -> x0, blocking collectives: 9.29 us -> none  [shards(): lax.all_to_all(returned, 'ma', split_axis=0, concat_axis=1, tiled=True)]
    all_to_all x1 -> x0, starting transfers between devices: 7.31 us -> none  [shards(): lax.all_to_all(fields, 'ma', split_axis=1, concat_axis=0, tiled=True)]
  transfers between devices with their start and end apart: 4 -> 3, of which waited for: 4 -> 0; matrix products, arithmetic and copies ran while one was open for 15% -> 11% of each run, Pallas kernels for 0% -> 19%
where the time goes in v1:
time: 99.9 us; the launch traced here: 99.3 us
  Pallas kernels  65.4 us (65%)
  local copies, waits for them, and re-layouts  18.4 us (18%)
  matrix products  7.7 us (8%)
  starting transfers between devices  4.43 us (4%)
  other arithmetic  1.71 us (2%)
  between operations  1.61 us (2%)
    pallas_call x1, Pallas kernels, sum_over_devices(): pl.pallas_call(functools.partial(sum_kernel, n_vert, count), out_shape=ja...  21 us
    pallas_call x1, Pallas kernels, finish_ritz(): pl.pallas_call(functools.partial(factor_kernel, float(coefficients)), out...  19.9 us
    pallas_call x1, Pallas kernels, transform(): pl.pallas_call(functools.partial(transform_kernel, n_ma, n_vert, min(colu...  15.1 us
    unnamed x14, local copies, waits for them, and re-layouts  9.01 us
    pallas_call x1, Pallas kernels, gram_terms(): pl.pallas_call(functools.partial(gram_kernel, n_vert), grid_spec=pltpu.Pr...  5.77 us
    dot_general x1, matrix products, shards(): jnp.einsum('km,scml->kscl', mix_rows, applied, preferred_element_type=F32)  4.62 us
    ppermute x3, starting transfers between devices, shards(): received.append(lax.ppermute(piece, 'vert', ring))  4.43 us
    pallas_call x1, Pallas kernels, apply_tables(): pl.pallas_call(applied_kernel, grid=(orders,), out_shape=jax.ShapeDtypeSt...  3.73 us
  transfers between devices with their start and end apart: 3, of which 0 were waited for; matrix products, arithmetic and copies ran while one was open for 11% of the time, Pallas kernels for 19%

profile of v1, /device:TPU:0, one launch (start us, length us, event | category | flops | bytes accessed | tf_op | source)
XLA Modules:
  0.0 99.3 jit_solution(4324631931680289037)
XLA Ops:
  0.6 0.0 copy-start
  0.7 2.8 %copy.35 = bf16[32,8,4,1024]{3,0,2,1:T(8,128)(2,1)S(1)} copy(bf16[32,8,4,1024]{3,2,1,0:T(4,128)(2,1)} %param.6) | data formatting | bytes 4194304 | tf_op args[0]
  3.5 0.0 copy-start.3
  3.5 0.0 copy-start.4
  3.6 0.0 copy-start.5
  3.6 0.0 copy-start.2
  3.6 1.2 %dynamic-slice_bitcast_fusion = (bf16[2,4,32,1024]{3,2,1,0:T(8,128)(2,1)}, bf16[2,4,32,1024]{3,2,1,0:T(8,128)(2,1)}, bf16[2,4,32,1024]{3,2,1,0:T(8,128)(2,1)}) fusion(bf16[32,8,4,1024]{3,0,2,1:T(8,128)(2,1)S(1)} %copy.35, s32[]{:T(128)S(6)} %select_n.73, s32[]{:T(128)S(6)} %select_n.71, s32[]{:T(128)S(6)} %select_n.69), kind=kLoop, calls=%fused_computation.1 | loop fusion | bytes 3145740 | tf_op jit(solution)/shard_map/dynamic_slice | solution.py:388
  4.8 0.5 collective-permute-start.2
  5.3 2.5 %collective-permute-start.1 = (bf16[2,4,32,1024]{3,2,1,0:T(8,128)(2,1)}, bf16[2,4,32,1024]{3,2,1,0:T(8,128)(2,1)}, u32[]{:S(2)}, u32[]{:S(2)}) collective-permute-start(bf16[2,4,32,1024]{3,2,1,0:T(8,128)(2,1)} %get-tuple-element.13), channel_id=1, source_target_pairs={{0,2},{1,3},{2,0},{3,1},{4,6},{5,7},{6,4},{7,5},{8,10},{9,11},{10,... | collective-permute-start | bytes 1572872 | tf_op jit(solution)/shard_map/ppermute | solution.py:389
  7.8 1.5 %collective-permute-start = (bf16[2,4,32,1024]{3,2,1,0:T(8,128)(2,1)}, bf16[2,4,32,1024]{3,2,1,0:T(8,128)(2,1)}, u32[]{:S(2)}, u32[]{:S(2)}) collective-permute-start(bf16[2,4,32,1024]{3,2,1,0:T(8,128)(2,1)} %get-tuple-element.14), channel_id=1, source_target_pairs={{0,3},{1,0},{2,1},{3,2},{4,7},{5,4},{6,5},{7,6},{8,11},{9,8},{10,9... | collective-permute-start | bytes 1572872 | tf_op jit(solution)/shard_map/ppermute | solution.py:389
  9.2 0.0 copy-done.3
  9.2 0.7 compare_reduce_fusion
  10.7 0.1 dynamic_slice.34
  10.7 0.0 copy-done.4
  10.7 0.1 dynamic_slice.35
  10.8 0.0 copy-done.5
  10.8 0.1 dynamic_slice.33
  10.9 0.0 copy-done.2
  10.9 0.1 mul.87
  11.0 0.2 multiply_convert_fusion.1
  11.2 0.7 copy.21.table_ref
  11.9 0.1 fusion.20
  12.1 0.8 copy.22.factor_ref
  12.9 0.0 copy-done
  12.9 3.1 %fusion = f32[8,16,4,32]{3,1,2,0:T(8,128)S(1)} fusion(bf16[8,2,32,1024]{3,2,1,0:T(8,128)(2,1)S(1)} %copy-done, s32[]{:T(128)S(6)} %select_n.74, bf16[32,8,4,1024]{3,2,1,0:T(4,128)(2,1)} %param.6), kind=kOutput, calls=%fused_computation.4 | convolution fusion | flops 33554432 | bytes 2424836 | tf_op jit(solution)/shard_map/dot_general | solution.py:391
  16.1 0.1 copy.20
  16.1 0.7 convert_element_type.43.own_ref
  16.8 0.6 fusion.22.back_ref
  17.4 15.1 %transform.1 = bf16[4,16,512]{2,1,0:T(8,128)(2,1)} custom-call(bf16[16,512]{1,0:T(8,128)(2,1)} %convert_element_type.43.own_ref, bf16[128,128]{1,0:T(8,128)(2,1)} %copy.21.table_ref, bf16[16,128]{1,0:T(8,128)(2,1)} %fusion.22.back_ref, f32[128,512]{1,0:T(8,128)} %copy.22.factor_ref), custom_call_target="tpu_custom_call" | custom-call | tf_op jit(solution)/shard_map/transform/pallas_call | solution.py:110
  32.5 1.0 %reshape.166 = bf16[4,2,8,8,2,32]{5,4,3,2,1,0:T(2,128)(2,1)S(1)} reshape(bf16[4,16,512]{2,1,0:T(8,128)(2,1)} %transform.1) | data formatting | bytes 131072 | tf_op jit(solution)/shard_map/reshape | solution.py:422
  33.5 0.9 copy.34
  34.4 1.2 %reshape.167.g_ref = bf16[8,4,8,128]{3,2,1,0:T(8,128)(2,1)S(1)} reshape(bf16[8,2,2,8,4,32]{5,4,3,2,1,0:T(4,128)(2,1)} %bitcast.39) | data formatting | bytes 131072 | tf_op jit(solution)/shard_map/reshape | solution.py:423
  35.6 0.1 dynamic-slice_bitcast_fusion.3.table_ref
  35.7 3.7 %apply_tables.1.refs_4_ = bf16[8,4,128,1024]{3,2,1,0:T(8,128)(2,1)S(1)} custom-call(bf16[8,4,8,128]{3,2,1,0:T(8,128)(2,1)S(1)} %reshape.167.g_ref, bf16[8,16,1024]{2,1,0:T(8,128)(2,1)S(1)} %dynamic-slice_bitcast_fusion.3.table_ref), custom_call_target="tpu_custom_call" | custom-call | flops 1073741824 | bytes 8388608 | tf_op jit(solution)/shard_map/apply_tables/pallas_call | solution.py:144
  39.5 0.0 collective-permute-done.2.refs_3_
  39.5 0.0 collective-permute-done.1.refs_2_
  39.5 0.0 collective-permute-done.refs_1_
  39.5 5.8 %gram_terms.1 = f32[3,128,128]{2,1,0:T(8,128)S(1)} custom-call(s32[1]{0:T(128)} %bitcast.at_ref, bf16[8,4,32,1024]{3,2,1,0:T(8,128)(2,1)S(1)} %bitcast.38, bf16[2,4,32,1024]{3,2,1,0:T(8,128)(2,1)} %collective-permute-done.refs_1_, bf16[2,4,32,1024]{3,2,1,0:T(8,128)(2,1)} %collective-permute-done.1.refs_2_, ...), custom_call_target="tpu_custom_call" | custom-call | flops 1610612736 | bytes 4194304 | tf_op jit(solution)/shard_map/gram_terms/pallas_call | solution.py:191
  45.3 0.0 copy-start.1
  45.3 3.2 %copy-done.1 = bf16[8,4,128,1024]{3,2,1,0:T(8,128)(2,1)} copy-done((bf16[8,4,128,1024]{3,2,1,0:T(8,128)(2,1)}, bf16[8,4,128,1024]{3,2,1,0:T(8,128)(2,1)S(1)}, u32[]{:S(2)}) %copy-start.1) | copy-done | bytes 8388632
  48.5 0.7 reshape_reshape.6.part_ref
  49.2 21.0 %sum_over_devices.1 = f32[32,12,128]{2,1,0:T(8,128)} custom-call(f32[32,12,128]{2,1,0:T(8,128)} %reshape_reshape.6.part_ref), custom_call_target="tpu_custom_call" | custom-call | tf_op jit(solution)/shard_map/sum_over_devices/pallas_call | solution.py:282
  70.2 1.6 %reshape_reshape.7.totals_ref = f32[3,128,128]{2,1,0:T(8,128)} reshape(f32[32,12,128]{2,1,0:T(8,128)} %sum_over_devices.1) | data formatting | bytes 393216 | tf_op jit(solution)/shard_map/reshape;reshape | solution.py:291
  71.8 19.9 %finish_ritz.1 = (f32[128,128]{1,0:T(8,128)}, bf16[128,128]{1,0:T(8,128)(2,1)}) custom-call(f32[3,128,128]{2,1,0:T(8,128)} %reshape_reshape.7.totals_ref), custom_call_target="tpu_custom_call" | custom-call | tf_op jit(solution)/shard_map/finish_ritz/pallas_call | solution.py:347
  91.7 4.6 %convolution_convert_fusion = bf16[32,8,4,1024]{3,0,2,1:T(8,128)(2,1)S(1)} fusion(bf16[8,4,128,1024]{3,2,1,0:T(8,128)(2,1)} %copy-done.1, bf16[128,128]{1,0:T(8,128)(2,1)} %get-tuple-element.6, s32[]{:T(128)S(6)} %select_n.78), kind=kOutput, calls=%fused_computation | convolution fusion | flops 269484032 | bytes 10493956 | tf_op jit(solution)/shard_map/km,scml->kscl/dot_general | solution.py:430
  96.4 2.9 %copy.24 = bf16[32,8,4,1024]{3,2,1,0:T(4,128)(2,1)} copy(bf16[32,8,4,1024]{3,0,2,1:T(8,128)(2,1)S(1)} %convolution_convert_fusion) | data formatting | bytes 4194304
  (5 shorter events, 0.1 us)
Async XLA Ops:
  0.6 12.3 %copy-start = (bf16[8,2,32,1024]{3,2,1,0:T(8,128)(2,1)S(1)}, bf16[8,2,32,1024]{3,2,1,0:T(8,128)(2,1)}, u32[]{:S(2)}) copy-start(bf16[8,2,32,1024]{3,2,1,0:T(8,128)(2,1)} %param.7) | copy-start | bytes 3145732
  3.5 5.7 %copy-start.3 = (s32[32]{0:T(128)S(1)}, s32[32]{0:T(128)}, u32[]{:S(2)}) copy-start(s32[32]{0:T(128)} %param.10) | copy-start | bytes 388
  3.5 7.2 %copy-start.4 = (f32[32]{0:T(128)S(1)}, f32[32]{0:T(128)}, u32[]{:S(2)}) copy-start(f32[32]{0:T(128)} %param.11) | copy-start | bytes 388
  3.6 7.3 %copy-start.5 = (s32[32]{0:T(128)S(1)}, s32[32]{0:T(128)}, u32[]{:S(2)}) copy-start(s32[32]{0:T(128)} %param.9) | copy-start | bytes 388
  3.6 7.3 %copy-start.2 = (s32[64]{0:T(128)S(1)}, s32[64]{0:T(128)}, u32[]{:S(2)}) copy-start(s32[64]{0:T(128)} %param.8) | copy-start | bytes 772
  4.8 34.7 %collective-permute-start.2 = (bf16[2,4,32,1024]{3,2,1,0:T(8,128)(2,1)}, bf16[2,4,32,1024]{3,2,1,0:T(8,128)(2,1)}, u32[]{:S(2)}, u32[]{:S(2)}) collective-permute-start(bf16[2,4,32,1024]{3,2,1,0:T(8,128)(2,1)} %get-tuple-element.12), channel_id=1, source_target_pairs={{0,1},{1,2},{2,3},{3,0},{4,5},{5,6},{6,7},{7,4},{8,9},{9,10},{10,1... | collective-permute-start | bytes 1572872 | tf_op jit(solution)/shard_map/ppermute | solution.py:389
  5.3 34.2 %collective-permute-start.1 = (bf16[2,4,32,1024]{3,2,1,0:T(8,128)(2,1)}, bf16[2,4,32,1024]{3,2,1,0:T(8,128)(2,1)}, u32[]{:S(2)}, u32[]{:S(2)}) collective-permute-start(bf16[2,4,32,1024]{3,2,1,0:T(8,128)(2,1)} %get-tuple-element.13), channel_id=1, source_target_pairs={{0,2},{1,3},{2,0},{3,1},{4,6},{5,7},{6,4},{7,5},{8,10},{9,11},{10,... | collective-permute-start | bytes 1572872 | tf_op jit(solution)/shard_map/ppermute | solution.py:389
  7.8 31.7 %collective-permute-start = (bf16[2,4,32,1024]{3,2,1,0:T(8,128)(2,1)}, bf16[2,4,32,1024]{3,2,1,0:T(8,128)(2,1)}, u32[]{:S(2)}, u32[]{:S(2)}) collective-permute-start(bf16[2,4,32,1024]{3,2,1,0:T(8,128)(2,1)} %get-tuple-element.14), channel_id=1, source_target_pairs={{0,3},{1,0},{2,1},{3,2},{4,7},{5,4},{6,5},{7,6},{8,11},{9,8},{10,9... | collective-permute-start | bytes 1572872 | tf_op jit(solution)/shard_map/ppermute | solution.py:389
  45.3 3.2 %copy-start.1 = (bf16[8,4,128,1024]{3,2,1,0:T(8,128)(2,1)}, bf16[8,4,128,1024]{3,2,1,0:T(8,128)(2,1)S(1)}, u32[]{:S(2)}) copy-start(bf16[8,4,128,1024]{3,2,1,0:T(8,128)(2,1)S(1)} %apply_tables.1.refs_4_) | copy-start | bytes 25165828

commit v2 on v1

--- a/solution.py
+++ b/solution.py
@@ -126,90 +126,108 @@
     )(own, table, back, factor)
 
 
-def applied_kernel(g_ref, table_ref, out_ref):
-    table = table_ref[0]
-    g = [g_ref[0, part].astype(F32) for part in range(4)]
+def applied_parts(g, table):
+    g = [part.astype(F32) for part in g]
     pairs = [(g[0], -g[3]), (g[1], g[2]), (-g[2], -g[1]), (-g[3], g[0])]
-    for part, (first, second) in enumerate(pairs):
+    blocks = []
+    for first, second in pairs:
         adjoint = jnp.concatenate([first, second], axis=0).astype(BF16)
         out = lax.dot_general(
             adjoint, table, (((0,), (0,)), ((), ())), preferred_element_type=F32
         )
-        out_ref[0, part] = out.astype(BF16)
-
-
-def apply_tables(g, table):
-    orders, parts, cycles, vectors = g.shape
-    depth, degrees = table.shape[1:]
-    return pl.pallas_call(
-        applied_kernel,
-        grid=(orders,),
-        out_shape=jax.ShapeDtypeStruct((orders, parts, vectors, degrees), BF16),
-        in_specs=[
-            pl.BlockSpec((1, parts, cycles, vectors), lambda s: (s, 0, 0, 0)),
-            pl.BlockSpec((1, depth, degrees), lambda s: (s, 0, 0)),
-        ],
-        out_specs=pl.BlockSpec((1, parts, vectors, degrees), lambda s: (s, 0, 0, 0)),
-        compiler_params=pltpu.CompilerParams(vmem_limit_bytes=32 * 1024 * 1024),
-        cost_estimate=pl.CostEstimate(
-            flops=16 * orders * parts * vectors * degrees * depth,
-            bytes_accessed=orders * parts * vectors * degrees * 2,
-            transcendentals=0,
-        ),
-        name="apply_tables",
-    )(g, table)
-
-
-def gram_kernel(n_vert, at_ref, *refs):
-    pieces = refs[:n_vert]
-    applied_ref, out_ref, trial = refs[n_vert], refs[n_vert + 1], refs[n_vert + 2]
+        blocks.append(out.astype(BF16))
+    return blocks
+
+
+def gram_kernel(n_vert, sizes, at_ref, own_ref, g_ref, table_ref, *refs):
+    pieces, out_ref, stack = refs[: sum(sizes)], refs[sum(sizes)], refs[sum(sizes) + 1]
     vert = at_ref[0]
-    vectors = pieces[0].shape[3 - 1]
-    first = (pl.program_id(0) == 0) & (pl.program_id(1) == 0)
-    for step in range(n_vert):
-        place = lax.rem(vert + step, n_vert)
-        trial[pl.ds(pl.multiple_of(place * vectors, vectors), vectors), :] = pieces[step][0, 0]
-
-    @pl.when(first)
-    def _():
-        out_ref[...] = jnp.zeros_like(out_ref)
-
+    share, parts, vectors, _ = own_ref.shape
+    total = n_vert * vectors
     dims = (((1,), (1,)), ((), ()))
-    t = trial[...]
-    a = applied_ref[0, 0]
-    out_ref[0] += lax.dot_general(t, t, dims, preferred_element_type=F32)
-    out_ref[1] += lax.dot_general(t, a, dims, preferred_element_type=F32)
-    out_ref[2] += lax.dot_general(a, a, dims, preferred_element_type=F32)
-
-
-def gram_terms(at, own, received, applied, n_vert):
+    sums = jnp.zeros((2 * total, 2 * total), F32)
+    for s in range(share):
+        applied = applied_parts([g_ref[s, part] for part in range(parts)], table_ref[s])
+        for part in range(parts):
+            buffer = stack.at[part % 2]
+            buffer[pl.ds(pl.multiple_of(vert * vectors, vectors), vectors), :] = own_ref[s, part]
+            taken = 0
+            for step in range(1, n_vert):
+                count = sizes[step - 1]
+                each = share // count
+                ref = pieces[taken + s // each]
+                taken += count
+                place = lax.rem(vert + step, n_vert)
+                rows = pl.ds(pl.multiple_of(place * vectors, vectors), vectors)
+                buffer[rows, :] = ref[s % each, part]
+            buffer[total:, :] = applied[part]
+            both = buffer[...]
+            sums += lax.dot_general(both, both, dims, preferred_element_type=F32)
+    out_ref[0] = sums[:total, :total]
+    out_ref[1] = sums[:total, total:]
+    out_ref[2] = sums[total:, total:]
+
+
+def gram_terms(at, own, g, table, received, n_vert):
     orders, parts, vectors, degrees = own.shape
     share = orders // n_vert
     total = n_vert * vectors
-    block = (1, 1, vectors, degrees)
-    flops = 12 * share * parts * total * total * degrees
+    sizes = [len(pieces) for pieces in received]
+    pieces = [piece for group in received for piece in group]
+    here = lambda i, at: (at[0], 0, 0, 0)
     return pl.pallas_call(
-        functools.partial(gram_kernel, n_vert),
+        functools.partial(gram_kernel, n_vert, sizes),
         grid_spec=pltpu.PrefetchScalarGridSpec(
             num_scalar_prefetch=1,
-            grid=(share, parts),
-            in_specs=[pl.BlockSpec(block, lambda s, c, at: (at[0] * share + s, c, 0, 0))]
-            + [pl.BlockSpec(block, lambda s, c, at: (s, c, 0, 0))] * (n_vert - 1)
-            + [
-                pl.BlockSpec(
-                    (1, 1, total, degrees), lambda s, c, at: (at[0] * share + s, c, 0, 0)
-                )
-            ],
-            out_specs=pl.BlockSpec((3, total, total), lambda s, c, at: (0, 0, 0)),
-            scratch_shapes=[VMEM((total, degrees), BF16)],
+            grid=(1,),
+            in_specs=[
+                pl.BlockSpec((share,) + own.shape[1:], here),
+                pl.BlockSpec((share,) + g.shape[1:], here),
+                pl.BlockSpec((share,) + table.shape[1:], lambda i, at: (at[0], 0, 0)),
+            ]
+            + [pl.BlockSpec(piece.shape, lambda i, at: (0, 0, 0, 0)) for piece in pieces],
+            out_specs=pl.BlockSpec((3, total, total), lambda i, at: (0, 0, 0)),
+            scratch_shapes=[VMEM((2, 2 * total, degrees), BF16)],
         ),
         out_shape=jax.ShapeDtypeStruct((3, total, total), F32),
         compiler_params=pltpu.CompilerParams(vmem_limit_bytes=32 * 1024 * 1024),
         cost_estimate=pl.CostEstimate(
-            flops=flops, bytes_accessed=4 * share * parts * total * degrees, transcendentals=0
+            flops=12 * share * parts * total * total * degrees,
+            bytes_accessed=4 * share * parts * total * degrees,
+            transcendentals=0,
         ),
         name="gram_terms",
-    )(at, own, *received, applied)
+    )(at, own, g, table, *pieces)
+
+
+def mix_kernel(mix_ref, g_ref, table_ref, out_ref, applied):
+    parts, _, total = g_ref.shape[1:]
+    vectors, _, _, degrees = out_ref.shape
+    blocks = applied_parts([g_ref[0, part] for part in range(parts)], table_ref[0])
+    for part, block in enumerate(blocks):
+        applied[part * total : (part + 1) * total, :] = block
+    mixed = jnp.dot(mix_ref[...], applied[...], preferred_element_type=F32)
+    out_ref[:, 0] = mixed.reshape(vectors, parts, degrees).astype(BF16)
+
+
+def mix(spread, g, table):
+    orders, parts, cycles, total = g.shape
+    depth, degrees = table.shape[1:]
+    vectors = spread.shape[0] // parts
+    return pl.pallas_call(
+        mix_kernel,
+        grid=(orders,),
+        out_shape=jax.ShapeDtypeStruct((vectors, orders, parts, degrees), BF16),
+        in_specs=[
+            pl.BlockSpec(spread.shape, lambda s: (0, 0)),
+            pl.BlockSpec((1, parts, cycles, total), lambda s: (s, 0, 0, 0)),
+            pl.BlockSpec((1, depth, degrees), lambda s: (s, 0, 0)),
+        ],
+        out_specs=pl.BlockSpec((vectors, 1, parts, degrees), lambda s: (0, s, 0, 0)),
+        scratch_shapes=[VMEM((parts * total, degrees), BF16)],
+        compiler_params=pltpu.CompilerParams(vmem_limit_bytes=32 * 1024 * 1024),
+        name="mix",
+    )(spread, g, table)
 
 
 def sum_kernel(n_vert, count, part_ref, out_ref, landed, send_a, recv_a, send_b, recv_b):
@@ -293,7 +311,7 @@
 
 def factor_kernel(coefficients, totals_ref, ritz_ref, mixing_ref, work):
     size = ritz_ref.shape[0]
-    panel = 8
+    panel = 16
     scale = 1.0 / coefficients
     row_at = lax.broadcasted_iota(jnp.int32, (size, size), 0)
     column_at = lax.broadcasted_iota(jnp.int32, (size, size), 1)
@@ -309,16 +327,23 @@
         first = pl.multiple_of(p * panel, panel)
         at = pl.ds(first, panel)
         panels = [work[b, at, :] for b in range(2)]
+        columns = [
+            [
+                jnp.sum(jnp.where(lane == first + i, x[:, :size], 0.0), axis=1, keepdims=True)
+                for i in range(panel)
+            ]
+            for x in panels
+        ]
         for i in range(panel):
             for b in range(2):
                 x = panels[b]
-                column = jnp.sum(
-                    jnp.where(lane == first + i, x[:, :size], 0.0), axis=1, keepdims=True
-                )
-                inverse = lax.rsqrt(column[i : i + 1, :])
+                column = columns[b]
+                inverse = lax.rsqrt(column[i][i : i + 1, :])
+                scaled = column[i] * inverse
+                for k in range(i + 1, panel):
+                    column[k] = column[k] - scaled * (column[k][i : i + 1, :] * inverse)
                 line = x[i : i + 1, :] * inverse
-                lower = x - (column * inverse) * line
-                panels[b] = jnp.where(sub == i, line, jnp.where(sub > i, lower, x))
+                panels[b] = jnp.where(sub == i, line, jnp.where(sub > i, x - scaled * line, x))
         for b in range(2):
             x = panels[b]
             update = lax.dot_general(
@@ -381,12 +406,20 @@
     trial = trial_block.transpose(1, 2, 0, 3)
 
     share = orders // n_vert
-    received = []
-    for step in range(1, n_vert):
+
+    def piece_for(step, begin, count):
+        target = (vert - step) % n_vert
+        return lax.dynamic_slice_in_dim(trial, target * share + begin, count, 0)
+
+    def send(piece, step):
         ring = [(source, (source - step) % n_vert) for source in range(n_vert)]
-        target = (vert - step) % n_vert
-        piece = lax.dynamic_slice_in_dim(trial, target * share, share, 0)
-        received.append(lax.ppermute(piece, "vert", ring))
+        return lax.ppermute(piece, "vert", ring)
+
+    far = n_vert // 2
+    half = share // 2
+    received = {step: [send(piece_for(step, 0, share), step)] for step in range(1, n_vert) if step != far}
+    received[far] = [send(piece_for(far, 0, half), far)]
+    late = piece_for(far, half, share - half)
 
     products = lax.dot_general(
         table, trial, (((2,), (3,)), ((0,), (0,))), preferred_element_type=F32
@@ -419,16 +452,19 @@
     factor = factor.reshape(longitudes, live * 2 * vectors)
 
     returned = transform(own, tables, back, factor, n_ma, n_vert)
+    late, returned = lax.optimization_barrier((late, returned))
+    received[far].append(send(late, far))
     g = returned.reshape(n_vert, 2, orders, live, 2, vectors).transpose(2, 4, 1, 3, 0, 5)
     g = g.reshape(orders, 4, live, n_vert * vectors)
-    applied = apply_tables(g, table)
-
-    terms = gram_terms(vert[None].astype(jnp.int32), trial, received, applied, n_vert)
+
+    pieces = [received[step] for step in range(1, n_vert)]
+    terms = gram_terms(vert[None].astype(jnp.int32), trial, g, table, pieces, n_vert)
     totals = sum_over_devices(terms, n_ma, n_vert)
     ritz_matrix, mixing = finish_ritz(totals, orders_total * parts * degrees)
     mix_rows = lax.dynamic_slice_in_dim(mixing, vert * vectors, vectors, 0)
-    mixed = jnp.einsum("km,scml->kscl", mix_rows, applied, preferred_element_type=F32)
-    return (mixed.astype(BF16), ritz_matrix)
+    spread = mix_rows[:, None, None, :] * jnp.eye(parts, dtype=BF16)[None, :, :, None]
+    spread = spread.reshape(vectors * parts, parts * n_vert * vectors)
+    return (mix(spread, g, table), ritz_matrix)
 
 
 def solution(mesh):

time: 99.9 us -> 86.7 us (0.87)
  Pallas kernels: 65.4 us -> 51.2 us
  waiting for transfers between devices: 0.01 us -> 9 us
  matrix products: 7.7 us -> 3.08 us
  local copies, waits for them, and re-layouts: 18.4 us -> 15.3 us
    pallas_call x1, Pallas kernels: 19.9 us -> 8.33 us  [finish_ritz(): pl.pallas_call(functools.partial(factor_kernel, float(coefficients)), out...]
    ppermute x3 -> x4, waiting for transfers between devices: 0.01 us -> 9 us  [send(): return lax.ppermute(piece, 'vert', ring)]
    unnamed x14, local copies, waits for them, and re-layouts: 9.01 us -> 3.54 us
    dot_general x1 -> x0, matrix products: 4.62 us -> none  [shards(): jnp.einsum('km,scml->kscl', mix_rows, applied, preferred_element_type=F32)]
    pallas_call x1, Pallas kernels: 15.1 us -> 13.3 us  [transform(): pl.pallas_call(functools.partial(transform_kernel, n_ma, n_vert, min(colu...]
    pallas_call x1, Pallas kernels: 21 us -> 19.3 us  [sum_over_devices(): pl.pallas_call(functools.partial(sum_kernel, n_vert, count), out_shape=ja...]
    dynamic_slice x1 -> x3, local copies, waits for them, and re-layouts: 1.2 us -> 2.63 us  [the longest x2 1.94 us: piece_for(): return lax.dynamic_slice_in_dim(trial, target * share + begin, count, 0)]
    ppermute x3 -> x4, starting transfers between devices: 4.43 us -> 4.43 us  [send(): return lax.ppermute(piece, 'vert', ring)]
  transfers between devices with their start and end apart: 3 -> 4, of which waited for: 0 -> 2; matrix products, arithmetic and copies ran while one was open for 11% -> 13% of each run, Pallas kernels for 19% -> 15%
where the time goes in v2:
time: 86.7 us; the launch traced here: 86.3 us
  Pallas kernels  51.2 us (59%)
  local copies, waits for them, and re-layouts  15.3 us (18%)
  waiting for transfers between devices  9 us (10%)
  starting transfers between devices  4.43 us (5%)
  matrix products  3.08 us (4%)
  other arithmetic  1.78 us (2%)
  between operations  1.53 us (2%)
    pallas_call x1, Pallas kernels, sum_over_devices(): pl.pallas_call(functools.partial(sum_kernel, n_vert, count), out_shape=ja...  19.3 us
    pallas_call x1, Pallas kernels, transform(): pl.pallas_call(functools.partial(transform_kernel, n_ma, n_vert, min(colu...  13.3 us
    ppermute x4, waiting for transfers between devices, send(): return lax.ppermute(piece, 'vert', ring)  9 us
    pallas_call x1, Pallas kernels, finish_ritz(): pl.pallas_call(functools.partial(factor_kernel, float(coefficients)), out...  8.33 us
    pallas_call x1, Pallas kernels, mix(): pl.pallas_call(mix_kernel, grid=(orders,), out_shape=jax.ShapeDtypeStruct...  6.24 us
    ppermute x4, starting transfers between devices, send(): return lax.ppermute(piece, 'vert', ring)  4.43 us
    pallas_call x1, Pallas kernels, gram_terms(): pl.pallas_call(functools.partial(gram_kernel, n_vert, sizes), grid_spec=p...  3.95 us
    unnamed x14, local copies, waits for them, and re-layouts  3.54 us
  transfers between devices with their start and end apart: 4, of which 2 were waited for; matrix products, arithmetic and copies ran while one was open for 13% of the time, Pallas kernels for 15%

profile of v2, /device:TPU:0, one launch (start us, length us, event | category | flops | bytes accessed | tf_op | source)
XLA Modules:
  0.0 86.3 jit_solution(15102796049518079301)
XLA Ops:
  0.6 0.0 copy-start
  0.7 2.8 %copy.37 = bf16[32,8,4,1024]{3,0,2,1:T(8,128)(2,1)S(1)} copy(bf16[32,8,4,1024]{3,2,1,0:T(4,128)(2,1)} %param.6) | data formatting | bytes 4194304 | tf_op args[0]
  3.5 0.0 copy-start.3
  3.5 0.0 copy-start.4
  3.5 0.0 copy-start.5
  3.6 0.0 copy-start.2
  3.6 1.1 %dynamic-slice_bitcast_fusion = (bf16[2,4,32,1024]{3,2,1,0:T(8,128)(2,1)}, bf16[2,4,32,1024]{3,2,1,0:T(8,128)(2,1)}) fusion(bf16[32,8,4,1024]{3,0,2,1:T(8,128)(2,1)S(1)} %copy.37, s32[]{:T(128)S(6)} %select_n.83, s32[]{:T(128)S(6)} %select_n.80), kind=kLoop, calls=%fused_computation | loop fusion | bytes 2097160 | tf_op jit(solution)/shard_map/dynamic_slice | solution.py:412
  4.7 2.4 %collective-permute-start = (bf16[2,4,32,1024]{3,2,1,0:T(8,128)(2,1)}, bf16[2,4,32,1024]{3,2,1,0:T(8,128)(2,1)}, u32[]{:S(2)}, u32[]{:S(2)}) collective-permute-start(bf16[2,4,32,1024]{3,2,1,0:T(8,128)(2,1)} %get-tuple-element.13), channel_id=1, source_target_pairs={{0,3},{1,0},{2,1},{3,2},{4,7},{5,4},{6,5},{7,6},{8,11},{9,8},{10,9... | collective-permute-start | bytes 1572872 | tf_op jit(solution)/shard_map/ppermute | solution.py:416
  7.1 0.0 collective-permute-start.3
  7.1 0.0 copy-done.3
  7.1 0.7 compare_reduce_fusion
  8.4 0.1 dynamic_slice.35
  8.4 0.0 copy-done
  8.4 3.1 %fusion = f32[8,16,4,32]{3,1,2,0:T(8,128)S(1)} fusion(bf16[8,2,32,1024]{3,2,1,0:T(8,128)(2,1)S(1)} %copy-done, s32[]{:T(128)S(6)} %select_n.75, bf16[32,8,4,1024]{3,2,1,0:T(4,128)(2,1)} %param.6), kind=kOutput, calls=%fused_computation.2 | convolution fusion | flops 33554432 | bytes 2424836 | tf_op jit(solution)/shard_map/dot_general | solution.py:424
  11.6 0.0 copy-done.4
  11.6 0.1 dynamic_slice.34
  11.7 0.0 copy-done.5
  11.7 0.1 dynamic_slice.36
  11.7 0.0 copy-done.2
  11.7 0.1 mul.103
  11.8 0.2 multiply_convert_fusion.1
  12.1 0.1 fusion.18
  12.2 0.1 copy.18
  12.3 0.7 convert_element_type.47.own_ref
  13.0 0.8 copy.20.factor_ref
  13.9 0.7 copy.19.table_ref
  14.6 0.6 fusion.20.back_ref
  15.2 13.3 %transform.1 = bf16[4,16,512]{2,1,0:T(8,128)(2,1)} custom-call(bf16[16,512]{1,0:T(8,128)(2,1)} %convert_element_type.47.own_ref, bf16[128,128]{1,0:T(8,128)(2,1)} %copy.19.table_ref, bf16[16,128]{1,0:T(8,128)(2,1)} %fusion.20.back_ref, f32[128,512]{1,0:T(8,128)} %copy.20.factor_ref), custom_call_target="tpu_custom_call" | custom-call | tf_op jit(solution)/shard_map/transform/pallas_call | solution.py:110
  28.5 0.9 dynamic-slice_bitcast_fusion.2
  29.4 0.8 collective-permute-start.2
  30.1 1.2 %collective-permute-start.1 = (bf16[1,4,32,1024]{3,2,1,0:T(8,128)(2,1)}, bf16[1,4,32,1024]{3,2,1,0:T(8,128)(2,1)}, u32[]{:S(2)}, u32[]{:S(2)}) collective-permute-start(bf16[1,4,32,1024]{3,2,1,0:T(8,128)(2,1)} %get-tuple-element.14), channel_id=1, source_target_pairs={{0,2},{1,3},{2,0},{3,1},{4,6},{5,7},{6,4},{7,5},{8,10},{9,11},{10,... | collective-permute-start | bytes 786440 | tf_op jit(solution)/shard_map/ppermute | solution.py:416
  31.4 1.0 %reshape.179 = bf16[4,2,8,8,2,32]{5,4,3,2,1,0:T(2,128)(2,1)S(1)} reshape(bf16[4,16,512]{2,1,0:T(8,128)(2,1)} %transform.1) | data formatting | bytes 131072 | tf_op jit(solution)/shard_map/reshape | solution.py:457
  32.4 0.9 %copy.35 = bf16[4,2,8,8,2,32]{5,0,3,1,4,2:T(4,128)(2,1)} copy(bf16[4,2,8,8,2,32]{5,4,3,2,1,0:T(2,128)(2,1)S(1)} %reshape.179) | data formatting | bytes 131072 | tf_op jit(solution)/shard_map/reshape | solution.py:457
  33.3 1.2 %reshape.180.g_ref = bf16[8,4,8,128]{3,2,1,0:T(8,128)(2,1)S(1)} reshape(bf16[8,2,2,8,4,32]{5,4,3,2,1,0:T(4,128)(2,1)} %bitcast.41) | data formatting | bytes 131072 | tf_op jit(solution)/shard_map/reshape | solution.py:458
  34.5 0.1 dynamic-slice_bitcast_fusion.4.table_ref
  34.6 4.2 %collective-permute-done.2.refs_2_ = bf16[1,4,32,1024]{3,2,1,0:T(8,128)(2,1)} collective-permute-done((bf16[1,4,32,1024]{3,2,1,0:T(8,128)(2,1)}, bf16[1,4,32,1024]{3,2,1,0:T(8,128)(2,1)}, u32[]{:S(2)}, u32[]{:S(2)}) %collective-permute-start.2) | collective-permute-done | bytes 262176 | tf_op jit(solution)/shard_map/ppermute | solution.py:416
  38.8 4.8 %collective-permute-done.1.refs_1_ = bf16[1,4,32,1024]{3,2,1,0:T(8,128)(2,1)} collective-permute-done((bf16[1,4,32,1024]{3,2,1,0:T(8,128)(2,1)}, bf16[1,4,32,1024]{3,2,1,0:T(8,128)(2,1)}, u32[]{:S(2)}, u32[]{:S(2)}) %collective-permute-start.1) | collective-permute-done | bytes 262176 | tf_op jit(solution)/shard_map/ppermute | solution.py:416
  43.6 0.0 collective-permute-done.refs_0_
  43.6 0.0 collective-permute-done.3.refs_3_
  43.6 4.0 %gram_terms.1 = f32[3,128,128]{2,1,0:T(8,128)S(1)} custom-call(s32[1]{0:T(128)} %bitcast.at_ref, bf16[8,4,32,1024]{3,2,1,0:T(8,128)(2,1)S(1)} %bitcast.39, bf16[8,4,8,128]{3,2,1,0:T(8,128)(2,1)S(1)} %reshape.180.g_ref, bf16[8,16,1024]{2,1,0:T(8,128)(2,1)S(1)} %dynamic-slice_bitcast_fusion.4.table_ref, bf16[2,4,32,1024]{3,2,1,0:T(8,128)(2,1)} %collective-permute-done.refs_0_, ...), custom_call_target="tpu_custom_call" | custom-call | flops 1610612736 | bytes 4194304 | tf_op jit(solution)/shard_map/gram_terms/pallas_call | solution.py:178
  47.6 0.0 copy-start.1
  47.6 0.7 copy-done.1
  48.3 1.6 %reshape_reshape.6.part_ref = f32[32,12,128]{2,1,0:T(8,128)} reshape(f32[3,128,128]{2,1,0:T(8,128)} %copy-done.1) | data formatting | bytes 393216 | tf_op jit(solution)/shard_map/reshape;reshape | solution.py:299
  49.9 19.3 %sum_over_devices.1 = f32[32,12,128]{2,1,0:T(8,128)} custom-call(f32[32,12,128]{2,1,0:T(8,128)} %reshape_reshape.6.part_ref), custom_call_target="tpu_custom_call" | custom-call | tf_op jit(solution)/shard_map/sum_over_devices/pallas_call | solution.py:300
  69.2 1.6 %reshape_reshape.7.totals_ref = f32[3,128,128]{2,1,0:T(8,128)} reshape(f32[32,12,128]{2,1,0:T(8,128)} %sum_over_devices.1) | data formatting | bytes 393216 | tf_op jit(solution)/shard_map/reshape;reshape | solution.py:309
  70.9 8.3 %finish_ritz.1 = (f32[128,128]{1,0:T(8,128)}, bf16[128,128]{1,0:T(8,128)(2,1)}) custom-call(f32[3,128,128]{2,1,0:T(8,128)} %reshape_reshape.7.totals_ref), custom_call_target="tpu_custom_call" | custom-call | tf_op jit(solution)/shard_map/finish_ritz/pallas_call | solution.py:372
  79.2 0.7 constant_dynamic-slice_fusion
  79.9 0.1 broadcast_multiply_fusion
  80.1 6.2 %mix.1 = bf16[32,8,4,1024]{3,2,1,0:T(4,128)(2,1)} custom-call(bf16[128,512]{1,0:T(8,128)(2,1)S(1)} %bitcast.40, bf16[8,4,8,128]{3,2,1,0:T(8,128)(2,1)S(1)} %reshape.180.g_ref, bf16[8,16,1024]{2,1,0:T(8,128)(2,1)S(1)} %dynamic-slice_bitcast_fusion.4.table_ref), custom_call_target="tpu_custom_call" | custom-call | tf_op jit(solution)/shard_map/mix/pallas_call | solution.py:217
  (7 shorter events, 0.1 us)
Async XLA Ops:
  0.6 7.8 %copy-start = (bf16[8,2,32,1024]{3,2,1,0:T(8,128)(2,1)S(1)}, bf16[8,2,32,1024]{3,2,1,0:T(8,128)(2,1)}, u32[]{:S(2)}) copy-start(bf16[8,2,32,1024]{3,2,1,0:T(8,128)(2,1)} %param.7) | copy-start | bytes 3145732
  3.5 3.6 %copy-start.3 = (s32[32]{0:T(128)S(1)}, s32[32]{0:T(128)}, u32[]{:S(2)}) copy-start(s32[32]{0:T(128)} %param.10) | copy-start | bytes 388
  3.5 8.0 %copy-start.4 = (s32[32]{0:T(128)S(1)}, s32[32]{0:T(128)}, u32[]{:S(2)}) copy-start(s32[32]{0:T(128)} %param.9) | copy-start | bytes 388
  3.5 8.1 %copy-start.5 = (f32[32]{0:T(128)S(1)}, f32[32]{0:T(128)}, u32[]{:S(2)}) copy-start(f32[32]{0:T(128)} %param.11) | copy-start | bytes 388
  3.6 8.2 %copy-start.2 = (s32[64]{0:T(128)S(1)}, s32[64]{0:T(128)}, u32[]{:S(2)}) copy-start(s32[64]{0:T(128)} %param.8) | copy-start | bytes 772
  4.7 39.0 %collective-permute-start = (bf16[2,4,32,1024]{3,2,1,0:T(8,128)(2,1)}, bf16[2,4,32,1024]{3,2,1,0:T(8,128)(2,1)}, u32[]{:S(2)}, u32[]{:S(2)}) collective-permute-start(bf16[2,4,32,1024]{3,2,1,0:T(8,128)(2,1)} %get-tuple-element.13), channel_id=1, source_target_pairs={{0,3},{1,0},{2,1},{3,2},{4,7},{5,4},{6,5},{7,6},{8,11},{9,8},{10,9... | collective-permute-start | bytes 1572872 | tf_op jit(solution)/shard_map/ppermute | solution.py:416
  7.1 36.6 %collective-permute-start.3 = (bf16[2,4,32,1024]{3,2,1,0:T(8,128)(2,1)}, bf16[2,4,32,1024]{3,2,1,0:T(8,128)(2,1)}, u32[]{:S(2)}, u32[]{:S(2)}) collective-permute-start(bf16[2,4,32,1024]{3,2,1,0:T(8,128)(2,1)} %get-tuple-element.12), channel_id=1, source_target_pairs={{0,1},{1,2},{2,3},{3,0},{4,5},{5,6},{6,7},{7,4},{8,9},{9,10},{10,1... | collective-permute-start | bytes 1572872 | tf_op jit(solution)/shard_map/ppermute | solution.py:416
  29.4 9.5 %collective-permute-start.2 = (bf16[1,4,32,1024]{3,2,1,0:T(8,128)(2,1)}, bf16[1,4,32,1024]{3,2,1,0:T(8,128)(2,1)}, u32[]{:S(2)}, u32[]{:S(2)}) collective-permute-start(bf16[1,4,32,1024]{3,2,1,0:T(8,128)(2,1)} %get-tuple-element.9), channel_id=1, source_target_pairs={{0,2},{1,3},{2,0},{3,1},{4,6},{5,7},{6,4},{7,5},{8,10},{9,11},{10,... | collective-permute-start | bytes 786440 | tf_op jit(solution)/shard_map/ppermute | solution.py:416
  30.1 13.5 %collective-permute-start.1 = (bf16[1,4,32,1024]{3,2,1,0:T(8,128)(2,1)}, bf16[1,4,32,1024]{3,2,1,0:T(8,128)(2,1)}, u32[]{:S(2)}, u32[]{:S(2)}) collective-permute-start(bf16[1,4,32,1024]{3,2,1,0:T(8,128)(2,1)} %get-tuple-element.14), channel_id=1, source_target_pairs={{0,2},{1,3},{2,0},{3,1},{4,6},{5,7},{6,4},{7,5},{8,10},{9,11},{10,... | collective-permute-start | bytes 786440 | tf_op jit(solution)/shard_map/ppermute | solution.py:416
  47.6 0.7 copy-start.1

commit v3 on v2

--- a/solution.py
+++ b/solution.py
@@ -7,6 +7,7 @@
 from jax.experimental import pallas as pl
 from jax.experimental.pallas import tpu as pltpu
 from jax.sharding import PartitionSpec as P
+
 
 MESH = pl.DeviceIdType.MESH
 VMEM = pltpu.VMEM
@@ -121,6 +122,9 @@
         ],
         compiler_params=pltpu.CompilerParams(
             collective_id=0, has_side_effects=True, vmem_limit_bytes=GRANT
+        ),
+        cost_estimate=pl.CostEstimate(
+            flops=20_000_000_000, bytes_accessed=2 * own.size * n_ma, transcendentals=0
         ),
         name="transform",
     )(own, table, back, factor)
@@ -230,12 +234,22 @@
     )(spread, g, table)
 
 
-def sum_kernel(n_vert, count, part_ref, out_ref, landed, send_a, recv_a, send_b, recv_b):
-    me = lax.axis_index("ma") * n_vert + lax.axis_index("vert")
+def sum_kernel(
+    n_vert, count, owners, part_ref, out_ref, landed, send_a, recv_a, send_b, recv_b
+):
+    ma = lax.axis_index("ma")
+    vert = lax.axis_index("vert")
+    slots = part_ref.shape[0]
+    me = ma * n_vert + vert
+    mine = jnp.where(vert < owners, lax.rem(ma * owners + vert, slots), 0)
+    owning = (vert < owners) & (ma * owners + vert < slots)
     barrier = pltpu.get_barrier_semaphore()
 
     def where(flat):
         return (flat // n_vert, lax.rem(flat, n_vert))
+
+    def owner(slot):
+        return slot // owners * n_vert + lax.rem(slot, owners)
 
     def greet(step, carry):
         other = lax.rem(me + step, count)
@@ -245,13 +259,13 @@
     lax.fori_loop(1, count, greet, 0)
     pl.semaphore_wait(barrier, count - 1)
 
-    def scatter(peer, slot):
+    def scatter(slot, source):
         return pltpu.make_async_remote_copy(
-            src_ref=part_ref.at[peer],
-            dst_ref=landed.at[slot],
-            send_sem=send_a.at[peer],
-            recv_sem=recv_a.at[slot],
-            device_id=where(peer),
+            src_ref=part_ref.at[slot],
+            dst_ref=landed.at[source],
+            send_sem=send_a.at[slot],
+            recv_sem=recv_a.at[source],
+            device_id=where(owner(slot)),
             device_id_type=MESH,
         )
 
@@ -265,48 +279,68 @@
             device_id_type=MESH,
         )
 
-    def exchange(copy):
-        def start(step, carry):
-            copy(lax.rem(me + step, count), me).start()
+    def over_slots(act):
+        def body(step, carry):
+            slot = lax.rem(ma * owners + vert + step, slots)
+
+            @pl.when(owner(slot) != me)
+            def _():
+                act(slot)
+
             return carry
 
-        def wait(step, carry):
-            other = lax.rem(me + step, count)
-            copy(other, me).wait_send()
-            copy(other, other).wait_recv()
+        lax.fori_loop(0, slots, body, 0)
+
+    def over_others(act):
+        def body(step, carry):
+            act(lax.rem(me + step, count))
             return carry
 
-        return start, wait
-
-    start, wait = exchange(scatter)
-    lax.fori_loop(1, count, start, 0)
-    landed[me] = part_ref[me]
-    lax.fori_loop(1, count, wait, 0)
-    out_ref[me] = jnp.sum(landed[...], axis=0)
-    start, wait = exchange(gather)
-    lax.fori_loop(1, count, start, 0)
-    lax.fori_loop(1, count, wait, 0)
+        lax.fori_loop(1, count, body, 0)
+
+    over_slots(lambda slot: scatter(slot, me).start())
+
+    @pl.when(owning)
+    def _():
+        landed[me] = part_ref[mine]
+        over_others(lambda other: scatter(mine, other).wait_recv())
+        out_ref[mine] = jnp.sum(landed[...], axis=0)
+        over_others(lambda other: gather(other, mine).start())
+
+    over_slots(lambda slot: scatter(slot, me).wait_send())
+    over_slots(lambda slot: gather(me, slot).wait_recv())
+
+    @pl.when(owning)
+    def _():
+        over_others(lambda other: gather(other, mine).wait_send())
 
 
 def sum_over_devices(terms, n_ma, n_vert):
     count = n_ma * n_vert
     lanes = terms.shape[-1]
     rows = terms.size // lanes
-    each = -(-rows // count)
-    flat = terms.reshape(rows, lanes)
-    if each * count != rows:
-        flat = jnp.pad(flat, ((0, each * count - rows), (0, 0)))
-    slots = flat.reshape(count, each, lanes)
+    each = 8
+    while rows % each or rows // each > count:
+        each *= 2
+    slots = rows // each
+    owners = slots // n_ma if slots % n_ma == 0 else n_vert
+    parts = terms.reshape(slots, each, lanes)
     out = pl.pallas_call(
-        functools.partial(sum_kernel, n_vert, count),
-        out_shape=jax.ShapeDtypeStruct(slots.shape, F32),
+        functools.partial(sum_kernel, n_vert, count, owners),
+        out_shape=jax.ShapeDtypeStruct(parts.shape, F32),
         in_specs=on_vmem(1),
         out_specs=pl.BlockSpec(memory_space=VMEM),
-        scratch_shapes=[VMEM(slots.shape, F32)] + [pltpu.SemaphoreType.DMA((count,))] * 4,
+        scratch_shapes=[
+            VMEM((count, each, lanes), F32),
+            pltpu.SemaphoreType.DMA((slots,)),
+            pltpu.SemaphoreType.DMA((count,)),
+            pltpu.SemaphoreType.DMA((count,)),
+            pltpu.SemaphoreType.DMA((slots,)),
+        ],
         compiler_params=pltpu.CompilerParams(collective_id=1, has_side_effects=True),
         name="sum_over_devices",
-    )(slots)
-    return out.reshape(each * count, lanes)[:rows].reshape(terms.shape)
+    )(parts)
+    return out.reshape(terms.shape)
 
 
 def factor_kernel(coefficients, totals_ref, ritz_ref, mixing_ref, work):
@@ -418,7 +452,8 @@
     far = n_vert // 2
     half = share // 2
     received = {step: [send(piece_for(step, 0, share), step)] for step in range(1, n_vert) if step != far}
-    received[far] = [send(piece_for(far, 0, half), far)]
+    early = piece_for(far, 0, half)
+    received[far] = [send(early, far)]
     late = piece_for(far, half, share - half)
 
     products = lax.dot_general(

time: 86.7 us -> 83.6 us (0.964)
  local copies, waits for them, and re-layouts: 15.3 us -> 12 us
    another operation x2 -> x0, local copies, waits for them, and re-layouts: 3.29 us -> none  [the longest x1 1.65 us: sum_over_devices(): slots = flat.reshape(count, each, lanes)]
  transfers between devices with their start and end apart: 4 -> 4, of which waited for: 2 -> 2; matrix products, arithmetic and copies ran while one was open for 13% -> 14% of each run, Pallas kernels for 15% -> 16%
where the time goes in v3:
time: 83.6 us; the launch traced here: 82.9 us
  Pallas kernels  51.1 us (61%)
  local copies, waits for them, and re-layouts  12 us (14%)
  waiting for transfers between devices  9 us (11%)
  starting transfers between devices  4.43 us (5%)
  matrix products  3.1 us (4%)
  other arithmetic  1.79 us (2%)
  between operations  1.5 us (2%)
    pallas_call x1, Pallas kernels, sum_over_devices(): pl.pallas_call(functools.partial(sum_kernel, n_vert, count, owners), out_...  19.2 us
    pallas_call x1, Pallas kernels, transform(): pl.pallas_call(functools.partial(transform_kernel, n_ma, n_vert, min(colu...  13.3 us
    ppermute x4, waiting for transfers between devices, send(): return lax.ppermute(piece, 'vert', ring)  9 us
    pallas_call x1, Pallas kernels, finish_ritz(): pl.pallas_call(functools.partial(factor_kernel, float(coefficients)), out...  8.34 us
    pallas_call x1, Pallas kernels, mix(): pl.pallas_call(mix_kernel, grid=(orders,), out_shape=jax.ShapeDtypeStruct...  6.24 us
    ppermute x4, starting transfers between devices, send(): return lax.ppermute(piece, 'vert', ring)  4.43 us
    pallas_call x1, Pallas kernels, gram_terms(): pl.pallas_call(functools.partial(gram_kernel, n_vert, sizes), grid_spec=p...  3.95 us
    unnamed x14, local copies, waits for them, and re-layouts  3.54 us
  transfers between devices with their start and end apart: 4, of which 2 were waited for; matrix products, arithmetic and copies ran while one was open for 14% of the time, Pallas kernels for 16%

profile of v3, /device:TPU:0, one launch (start us, length us, event | category | flops | bytes accessed | tf_op | source)
XLA Modules:
  0.0 82.9 jit_solution(13467894500999703273)
XLA Ops:
  0.6 0.0 copy-start
  0.7 2.8 %copy.37 = bf16[32,8,4,1024]{3,0,2,1:T(8,128)(2,1)S(1)} copy(bf16[32,8,4,1024]{3,2,1,0:T(4,128)(2,1)} %param.6) | data formatting | bytes 4194304 | tf_op args[0]
  3.5 0.0 copy-start.3
  3.5 1.1 %dynamic-slice_bitcast_fusion = (bf16[2,4,32,1024]{3,2,1,0:T(8,128)(2,1)}, bf16[2,4,32,1024]{3,2,1,0:T(8,128)(2,1)}) fusion(bf16[32,8,4,1024]{3,0,2,1:T(8,128)(2,1)S(1)} %copy.37, s32[]{:T(128)S(6)} %select_n.83, s32[]{:T(128)S(6)} %select_n.80), kind=kLoop, calls=%fused_computation | loop fusion | bytes 2097160 | tf_op jit(solution)/shard_map/dynamic_slice | solution.py:446
  4.6 0.0 copy-start.4
  4.6 0.0 copy-start.5
  4.6 2.4 %collective-permute-start = (bf16[2,4,32,1024]{3,2,1,0:T(8,128)(2,1)}, bf16[2,4,32,1024]{3,2,1,0:T(8,128)(2,1)}, u32[]{:S(2)}, u32[]{:S(2)}) collective-permute-start(bf16[2,4,32,1024]{3,2,1,0:T(8,128)(2,1)} %get-tuple-element.13), channel_id=1, source_target_pairs={{0,3},{1,0},{2,1},{3,2},{4,7},{5,4},{6,5},{7,6},{8,11},{9,8},{10,9... | collective-permute-start | bytes 1572872 | tf_op jit(solution)/shard_map/ppermute | solution.py:450
  7.0 0.0 collective-permute-start.3
  7.0 0.0 copy-done.3
  7.0 0.7 compare_reduce_fusion
  8.3 0.1 dynamic_slice.35
  8.4 0.0 copy-done
  8.4 0.0 copy-start.2
  8.4 3.1 %fusion = f32[8,16,4,32]{3,1,2,0:T(8,128)S(1)} fusion(bf16[8,2,32,1024]{3,2,1,0:T(8,128)(2,1)S(1)} %copy-done, s32[]{:T(128)S(6)} %select_n.75, bf16[32,8,4,1024]{3,2,1,0:T(4,128)(2,1)} %param.6), kind=kOutput, calls=%fused_computation.2 | convolution fusion | flops 33554432 | bytes 2424836 | tf_op jit(solution)/shard_map/dot_general | solution.py:459
  11.6 0.1 copy.18
  11.7 0.7 convert_element_type.47.own_ref
  12.4 0.0 copy-done.4
  12.4 0.1 dynamic_slice.34
  12.5 0.0 copy-done.5
  12.5 0.1 dynamic_slice.36
  12.5 0.1 fusion.18
  12.6 0.8 %copy.20.factor_ref = f32[128,512]{1,0:T(8,128)} copy(f32[128,512]{0,1:T(8,128)S(1)} %bitcast.45) | data formatting | bytes 524288 | tf_op jit(solution)/shard_map/reshape | solution.py:487
  13.5 0.0 copy-done.2
  13.5 0.1 mul.103
  13.6 0.2 multiply_convert_fusion.1
  13.8 0.6 fusion.20.back_ref
  14.4 0.7 copy.19.table_ref
  15.1 13.3 %transform.1 = bf16[4,16,512]{2,1,0:T(8,128)(2,1)} custom-call(bf16[16,512]{1,0:T(8,128)(2,1)} %convert_element_type.47.own_ref, bf16[128,128]{1,0:T(8,128)(2,1)} %copy.19.table_ref, bf16[16,128]{1,0:T(8,128)(2,1)} %fusion.20.back_ref, f32[128,512]{1,0:T(8,128)} %copy.20.factor_ref), custom_call_target="tpu_custom_call" | custom-call | flops 20000000000 | bytes 131072 | tf_op jit(solution)/shard_map/transform/pallas_call | solution.py:111
  28.5 0.9 %dynamic-slice_bitcast_fusion.2 = (bf16[1,4,32,1024]{3,2,1,0:T(8,128)(2,1)}, bf16[1,4,32,1024]{3,2,1,0:T(8,128)(2,1)}) fusion(bf16[32,8,4,1024]{3,0,2,1:T(8,128)(2,1)S(1)} %copy.37, s32[]{:T(128)S(6)} %select_n.81, s32[]{:T(128)S(6)} %select_n.74), kind=kLoop, calls=%fused_computation.5 | loop fusion | bytes 1048584 | tf_op jit(solution)/shard_map/dynamic_slice | solution.py:446
  29.3 0.8 collective-permute-start.2
  30.1 1.2 %collective-permute-start.1 = (bf16[1,4,32,1024]{3,2,1,0:T(8,128)(2,1)}, bf16[1,4,32,1024]{3,2,1,0:T(8,128)(2,1)}, u32[]{:S(2)}, u32[]{:S(2)}) collective-permute-start(bf16[1,4,32,1024]{3,2,1,0:T(8,128)(2,1)} %get-tuple-element.14), channel_id=1, source_target_pairs={{0,2},{1,3},{2,0},{3,1},{4,6},{5,7},{6,4},{7,5},{8,10},{9,11},{10,... | collective-permute-start | bytes 786440 | tf_op jit(solution)/shard_map/ppermute | solution.py:450
  31.4 1.0 %reshape.185 = bf16[4,2,8,8,2,32]{5,4,3,2,1,0:T(2,128)(2,1)S(1)} reshape(bf16[4,16,512]{2,1,0:T(8,128)(2,1)} %transform.1) | data formatting | bytes 131072 | tf_op jit(solution)/shard_map/reshape | solution.py:492
  32.4 0.9 %copy.35 = bf16[4,2,8,8,2,32]{5,0,3,1,4,2:T(4,128)(2,1)} copy(bf16[4,2,8,8,2,32]{5,4,3,2,1,0:T(2,128)(2,1)S(1)} %reshape.185) | data formatting | bytes 131072 | tf_op jit(solution)/shard_map/reshape | solution.py:492
  33.3 1.2 %reshape.186.g_ref = bf16[8,4,8,128]{3,2,1,0:T(8,128)(2,1)S(1)} reshape(bf16[8,2,2,8,4,32]{5,4,3,2,1,0:T(4,128)(2,1)} %bitcast.44) | data formatting | bytes 131072 | tf_op jit(solution)/shard_map/reshape | solution.py:493
  34.5 0.1 dynamic-slice_bitcast_fusion.4.table_ref
  34.6 4.2 %collective-permute-done.2.refs_2_ = bf16[1,4,32,1024]{3,2,1,0:T(8,128)(2,1)} collective-permute-done((bf16[1,4,32,1024]{3,2,1,0:T(8,128)(2,1)}, bf16[1,4,32,1024]{3,2,1,0:T(8,128)(2,1)}, u32[]{:S(2)}, u32[]{:S(2)}) %collective-permute-start.2) | collective-permute-done | bytes 262176 | tf_op jit(solution)/shard_map/ppermute | solution.py:450
  38.8 4.8 %collective-permute-done.1.refs_1_ = bf16[1,4,32,1024]{3,2,1,0:T(8,128)(2,1)} collective-permute-done((bf16[1,4,32,1024]{3,2,1,0:T(8,128)(2,1)}, bf16[1,4,32,1024]{3,2,1,0:T(8,128)(2,1)}, u32[]{:S(2)}, u32[]{:S(2)}) %collective-permute-start.1) | collective-permute-done | bytes 262176 | tf_op jit(solution)/shard_map/ppermute | solution.py:450
  43.6 0.0 collective-permute-done.refs_0_
  43.6 0.0 collective-permute-done.3.refs_3_
  43.6 3.9 %gram_terms.1 = f32[3,128,128]{2,1,0:T(8,128)S(1)} custom-call(s32[1]{0:T(128)} %bitcast.at_ref, bf16[8,4,32,1024]{3,2,1,0:T(8,128)(2,1)S(1)} %bitcast.41, bf16[8,4,8,128]{3,2,1,0:T(8,128)(2,1)S(1)} %reshape.186.g_ref, bf16[8,16,1024]{2,1,0:T(8,128)(2,1)S(1)} %dynamic-slice_bitcast_fusion.4.table_ref, bf16[2,4,32,1024]{3,2,1,0:T(8,128)(2,1)} %collective-permute-done.refs_0_, ...), custom_call_target="tpu_custom_call" | custom-call | flops 1610612736 | bytes 4194304 | tf_op jit(solution)/shard_map/gram_terms/pallas_call | solution.py:182
  47.6 0.0 copy-start.1
  47.6 0.7 copy-done.1
  48.2 19.2 %sum_over_devices.1 = f32[24,16,128]{2,1,0:T(8,128)} custom-call(f32[24,16,128]{2,1,0:T(8,128)} %bitcast.43), custom_call_target="tpu_custom_call" | custom-call | tf_op jit(solution)/shard_map/sum_over_devices/pallas_call | solution.py:328
  67.5 8.3 %finish_ritz.1 = (f32[128,128]{1,0:T(8,128)}, bf16[128,128]{1,0:T(8,128)(2,1)}) custom-call(f32[3,128,128]{2,1,0:T(8,128)} %bitcast.46), custom_call_target="tpu_custom_call" | custom-call | tf_op jit(solution)/shard_map/finish_ritz/pallas_call | solution.py:406
  75.8 0.7 constant_dynamic-slice_fusion
  76.5 0.1 broadcast_multiply_fusion
  76.7 6.2 %mix.1 = bf16[32,8,4,1024]{3,2,1,0:T(4,128)(2,1)} custom-call(bf16[128,512]{1,0:T(8,128)(2,1)S(1)} %bitcast.42, bf16[8,4,8,128]{3,2,1,0:T(8,128)(2,1)S(1)} %reshape.186.g_ref, bf16[8,16,1024]{2,1,0:T(8,128)(2,1)S(1)} %dynamic-slice_bitcast_fusion.4.table_ref), custom_call_target="tpu_custom_call" | custom-call | tf_op jit(solution)/shard_map/mix/pallas_call | solution.py:221
  (7 shorter events, 0.1 us)
Async XLA Ops:
  0.6 7.8 %copy-start = (bf16[8,2,32,1024]{3,2,1,0:T(8,128)(2,1)S(1)}, bf16[8,2,32,1024]{3,2,1,0:T(8,128)(2,1)}, u32[]{:S(2)}) copy-start(bf16[8,2,32,1024]{3,2,1,0:T(8,128)(2,1)} %param.7) | copy-start | bytes 3145732
  3.5 3.5 %copy-start.3 = (s32[32]{0:T(128)S(1)}, s32[32]{0:T(128)}, u32[]{:S(2)}) copy-start(s32[32]{0:T(128)} %param.10) | copy-start | bytes 388
  4.6 7.8 %copy-start.4 = (s32[32]{0:T(128)S(1)}, s32[32]{0:T(128)}, u32[]{:S(2)}) copy-start(s32[32]{0:T(128)} %param.9) | copy-start | bytes 388
  4.6 7.8 %copy-start.5 = (f32[32]{0:T(128)S(1)}, f32[32]{0:T(128)}, u32[]{:S(2)}) copy-start(f32[32]{0:T(128)} %param.11) | copy-start | bytes 388
  4.6 39.0 %collective-permute-start = (bf16[2,4,32,1024]{3,2,1,0:T(8,128)(2,1)}, bf16[2,4,32,1024]{3,2,1,0:T(8,128)(2,1)}, u32[]{:S(2)}, u32[]{:S(2)}) collective-permute-start(bf16[2,4,32,1024]{3,2,1,0:T(8,128)(2,1)} %get-tuple-element.13), channel_id=1, source_target_pairs={{0,3},{1,0},{2,1},{3,2},{4,7},{5,4},{6,5},{7,6},{8,11},{9,8},{10,9... | collective-permute-start | bytes 1572872 | tf_op jit(solution)/shard_map/ppermute | solution.py:450
  7.0 36.6 %collective-permute-start.3 = (bf16[2,4,32,1024]{3,2,1,0:T(8,128)(2,1)}, bf16[2,4,32,1024]{3,2,1,0:T(8,128)(2,1)}, u32[]{:S(2)}, u32[]{:S(2)}) collective-permute-start(bf16[2,4,32,1024]{3,2,1,0:T(8,128)(2,1)} %get-tuple-element.12), channel_id=1, source_target_pairs={{0,1},{1,2},{2,3},{3,0},{4,5},{5,6},{6,7},{7,4},{8,9},{9,10},{10,1... | collective-permute-start | bytes 1572872 | tf_op jit(solution)/shard_map/ppermute | solution.py:450
  8.4 5.1 %copy-start.2 = (s32[64]{0:T(128)S(1)}, s32[64]{0:T(128)}, u32[]{:S(2)}) copy-start(s32[64]{0:T(128)} %param.8) | copy-start | bytes 772
  29.3 9.5 %collective-permute-start.2 = (bf16[1,4,32,1024]{3,2,1,0:T(8,128)(2,1)}, bf16[1,4,32,1024]{3,2,1,0:T(8,128)(2,1)}, u32[]{:S(2)}, u32[]{:S(2)}) collective-permute-start(bf16[1,4,32,1024]{3,2,1,0:T(8,128)(2,1)} %get-tuple-element.9), channel_id=1, source_target_pairs={{0,2},{1,3},{2,0},{3,1},{4,6},{5,7},{6,4},{7,5},{8,10},{9,11},{10,... | collective-permute-start | bytes 786440 | tf_op jit(solution)/shard_map/ppermute | solution.py:450
  30.1 13.5 %collective-permute-start.1 = (bf16[1,4,32,1024]{3,2,1,0:T(8,128)(2,1)}, bf16[1,4,32,1024]{3,2,1,0:T(8,128)(2,1)}, u32[]{:S(2)}, u32[]{:S(2)}) collective-permute-start(bf16[1,4,32,1024]{3,2,1,0:T(8,128)(2,1)} %get-tuple-element.14), channel_id=1, source_target_pairs={{0,2},{1,3},{2,0},{3,1},{4,6},{5,7},{6,4},{7,5},{8,10},{9,11},{10,... | collective-permute-start | bytes 786440 | tf_op jit(solution)/shard_map/ppermute | solution.py:450
  47.6 0.7 copy-start.1
